TPU v7x, 256 devices: a whole 4x4x8 slice. The times are simulated.
256 devices in a mesh: gx: 8 (over z), gy: 32 (over y, x, core).
Axes of the slice: x: 4, y: 4, z: 8, core: 2. Of those that a mesh axis runs over, the one named last changes fastest.
Arguments:
- right_side: float32 [1024, 8192], P('gx', 'gy'), may hold values from -1.2 to 1.2
- shift: float32 [1024, 8192], P('gx', 'gy'), may hold values from 0.0001 to 0.004
Outputs:
- solution: float32 [1024, 8192], P('gx', 'gy')
- residual: float32 [1024, 8192], P('gx', 'gy')
All inputs are finite; a program needn't handle non-finite values.
Results may differ from a plain program's by a relative error of at most 0.0003.
Values sent between devices are 32-bit elements; how exact they have to be, the bound alone decides.
A program may use at most 128 MiB of HBM per device.

v0:
```python
import jax
import jax.numpy as jnp
from jax import lax
from jax.sharding import PartitionSpec as P

LEVELS = 4
COARSE_SWEEPS = 6


damping = 0.8


def extended(x, sides, width):
    edges = {}
    for axis, dim in sides:
        peers, length = (lax.axis_size(axis), x.shape[dim])
        up = [(i, (i + 1) % peers) for i in range(peers - 1)]
        last = lax.slice_in_dim(x, length - width, length, axis=dim)
        first = lax.slice_in_dim(x, 0, width, axis=dim)
        edges[dim] = (
            lax.ppermute(last, axis, up),
            lax.ppermute(first, axis, [(b, a) for a, b in up]),
        )
    done = []
    for _, dim in sides:
        low, high = edges[dim]
        around = [(width, width) if d in done else (0, 0) for d in range(x.ndim)]
        x = jnp.concatenate([jnp.pad(low, around), x, jnp.pad(high, around)], axis=dim)
        done.append(dim)
    return x


def padded_2(cells, sides, width):
    for axis, dim in sides:
        count = lax.axis_size(axis)
        ends = count - 1
        head = lax.slice_in_dim(cells, 0, width, axis=dim)
        tail = lax.slice_in_dim(cells, cells.shape[dim] - width, cells.shape[dim], axis=dim)
        cells = jnp.concatenate(
            [
                lax.ppermute(tail, axis, [(i, (i + 1) % count) for i in range(ends)]),
                cells,
                lax.ppermute(head, axis, [((i + 1) % count, i) for i in range(ends)]),
            ],
            axis=dim,
        )
    return cells


def in_order(pieces, dim):
    pieces = jnp.moveaxis(pieces, 0, dim)
    shape = pieces.shape
    return pieces.reshape(*shape[:dim], shape[dim] * shape[dim + 1], *shape[dim + 2 :])


def sent_to_all(x, axis):
    copies = jnp.broadcast_to(x, (lax.axis_size(axis), *x.shape))
    return lax.all_to_all(copies, axis, split_axis=0, concat_axis=0, tiled=True)


def gather_directly(x, axis, dim):
    return in_order(sent_to_all(x, axis), dim)


def restrict(values):
    rows, columns = values.shape
    blocks = values.reshape(rows // 2, 2, columns // 2, 2)
    return 0.25 * (
        blocks[:, 0, :, 0] + blocks[:, 1, :, 0] + blocks[:, 0, :, 1] + blocks[:, 1, :, 1]
    )


def prolong(values):
    rows, columns = values.shape
    copies = jnp.broadcast_to(values[:, None, :, None], (rows, 2, columns, 2))
    return copies.reshape(2 * rows, 2 * columns)


def operate_padded(padded, shifts, level):
    centre = padded[1:-1, 1:-1]
    beside = padded[2:, 1:-1] + padded[:-2, 1:-1] + padded[1:-1, 2:] + padded[1:-1, :-2]
    return 4.0 ** (-level) * (4.0 * centre - beside) + shifts * centre


def with_rim(field):
    return extended(field, (("gx", 0), ("gy", 1)), 1)


def inside_mask(rows, columns):
    row_ids = lax.axis_index("gx") * rows - 1 + jnp.arange(rows + 2, dtype=jnp.int32)
    col_ids = lax.axis_index("gy") * columns - 1 + jnp.arange(columns + 2, dtype=jnp.int32)
    row_ok = (row_ids >= 0) & (row_ids < rows * lax.axis_size("gx"))
    col_ok = (col_ids >= 0) & (col_ids < columns * lax.axis_size("gy"))
    return row_ok[:, None] & col_ok[None, :]


def build_levels(shift):
    levels = []
    shifts = shift
    for level in range(LEVELS + 1):
        diagonal = 4.0 ** (1 - level) + shifts
        outer_shift = None
        inside = None
        if level < LEVELS:
            outer_shift = padded_2(shifts, (("gx", 0), ("gy", 1)), 2)
            inside = inside_mask(shifts.shape[0], shifts.shape[1])
        levels.append((shifts, diagonal, outer_shift, inside))
        if level < LEVELS:
            shifts = restrict(shifts)
    return levels


def sweep_once(iterate, source, section, level):
    shifts, diagonal = (section[0], section[1])
    if iterate is None:
        return damping * source / diagonal
    return (
        iterate + damping * (source - operate_padded(with_rim(iterate), shifts, level)) / diagonal
    )


def sweep_pair(iterate, source, section, level):
    shifts, diagonal, outer_shift, inside = section
    if iterate is None:
        return sweep_once(sweep_once(None, source, section, level), source, section, level)
    stacked = padded_2(jnp.stack([iterate, source]), (("gx", 1), ("gy", 2)), 2)
    outer_iter = stacked[0]
    outer_source = stacked[1]
    inner_shift = outer_shift[1:-1, 1:-1]
    inner_diag = 4.0 ** (1 - level) + inner_shift
    first = (
        outer_iter[1:-1, 1:-1]
        + damping
        * (outer_source[1:-1, 1:-1] - operate_padded(outer_iter, inner_shift, level))
        / inner_diag
    )
    first = jnp.where(inside, first, 0.0)
    return first[1:-1, 1:-1] + damping * (source - operate_padded(first, shifts, level)) / diagonal


def smooth_two(iterate, source, section, level):
    return sweep_pair(iterate, source, section, level)


def residual_of(iterate, source, section, level):
    return source - operate_padded(with_rim(iterate), section[0], level)


def gather_whole(field):
    row_band = gather_directly(field, "gy", 1)
    return gather_directly(row_band, "gx", 0)


def local_sweeps(iterate, source, shifts, level, count):
    diagonal = 4.0 ** (1 - level) + shifts
    for turn in range(count):
        iterate = (
            iterate
            + damping * (source - operate_padded(jnp.pad(iterate, 1), shifts, level)) / diagonal
        )
    return iterate


def local_coarse(iterate, source, shifts):
    unit_total = jnp.sum(operate_padded(jnp.pad(jnp.ones_like(source), 1), shifts, LEVELS))
    if iterate is None:
        left = jnp.sum(source)
        iterate = jnp.zeros_like(source) + left / unit_total
    else:
        left = jnp.sum(source - operate_padded(jnp.pad(iterate, 1), shifts, LEVELS))
        iterate = iterate + left / unit_total
    return local_sweeps(iterate, source, shifts, LEVELS, COARSE_SWEEPS)


def own_block(whole, rows, columns):
    return lax.dynamic_slice(
        whole, (lax.axis_index("gx") * rows, lax.axis_index("gy") * columns), (rows, columns)
    )


def coarse_solve(coarse_rhs, shift_whole, twice):
    whole_rhs = gather_whole(coarse_rhs)
    whole = local_coarse(None, whole_rhs, shift_whole)
    if twice:
        whole = local_coarse(whole, whole_rhs, shift_whole)
    return own_block(whole, coarse_rhs.shape[0], coarse_rhs.shape[1])


def vcycle(level, iterate, source, levels, shift_whole):
    section = levels[level]
    iterate = smooth_two(iterate, source, section, level)
    coarse_rhs = restrict(residual_of(iterate, source, section, level))
    if level + 1 == LEVELS:
        correction = coarse_solve(coarse_rhs, shift_whole, False)
    else:
        correction = vcycle(level + 1, None, coarse_rhs, levels, shift_whole)
    iterate = iterate + prolong(correction)
    return smooth_two(iterate, source, section, level)


def fcycle(level, source, levels, shift_whole):
    section = levels[level]
    iterate = smooth_two(None, source, section, level)
    coarse_rhs = restrict(residual_of(iterate, source, section, level))
    if level + 1 == LEVELS:
        correction = coarse_solve(coarse_rhs, shift_whole, True)
    else:
        correction = fcycle(level + 1, coarse_rhs, levels, shift_whole)
        correction = vcycle(level + 1, correction, coarse_rhs, levels, shift_whole)
    iterate = iterate + prolong(correction)
    return smooth_two(iterate, source, section, level)


def body(right_side, shift):
    levels = build_levels(shift)
    shift_whole = gather_whole(levels[LEVELS][0])
    solution = fcycle(0, right_side, levels, shift_whole)
    residual = residual_of(solution, right_side, levels[0], 0)
    return (solution, residual)


def solution(mesh):
    in_specs = (P("gx", "gy"), P("gx", "gy"))
    out_specs = (P("gx", "gy"), P("gx", "gy"))
    return jax.shard_map(body, mesh=mesh, in_specs=in_specs, out_specs=out_specs, check_vma=False)
```

profile of v0, /device:TPU:104, one launch (start us, length us, event | category | flops | bytes accessed | tf_op | source)
XLA Modules:
  0.0 791.0 jit_solution(12912869299415072983)
XLA Ops:
  14.7 10.5 %reshape.552 = f32[64,2,128,2]{3,2,1,0:T(8,128)} reshape(f32[128,256]{1,0:T(8,128)} %param.3) | data formatting | bytes 262144 | tf_op jit(solution)/shard_map/reshape | solution.py:67
  25.2 9.1 %fusion.757 = (f32[64,128]{1,0:T(8,128)S(1)}, f32[64,1,128,1]{3,2,1,0:T(8,128)}) fusion(f32[64,2,128,2]{3,2,1,0:T(8,128)} %reshape.552), kind=kLoop, calls=%fused_computation.1319 | loop fusion | flops 32768 | bytes 196608 | tf_op jit(solution)/shard_map/mul | solution.py:68
  36.7 5.4 collective-permute-start.6
  53.4 9.8 %reshape.551 = f32[64,2,128,2]{3,2,1,0:T(8,128)} reshape(f32[128,256]{1,0:T(8,128)S(1)} %fusion.326) | data formatting | bytes 262144 | tf_op jit(solution)/shard_map/reshape | solution.py:67
  63.2 8.6 %multiply_reduce_fusion.1 = (f32[64,128]{1,0:T(8,128)S(1)}, f32[64,128]{1,0:T(8,128)S(1)}) fusion(f32[64,2,128,2]{3,2,1,0:T(8,128)} %reshape.551), kind=kLoop, calls=%fused_computation.8 | loop fusion | flops 40960 | bytes 196608 | tf_op jit(solution)/shard_map/mul | solution.py:116
  71.9 5.2 collective-permute-start.10
  80.9 5.1 collective-permute-start.9
  96.0 5.3 collective-permute-start.13
  114.6 5.1 collective-permute-start.17
  128.1 5.1 collective-permute-start.21
  135.1 8.5 %all-to-all-start.2 = ((f32[32,1,128]{2,1,0:T(1,128)}), f32[32,1,128]{2,1,0:T(1,128)S(1)}, u32[]{:S(2)}, u32[]{:S(2)}) async-start(f32[32,1,128]{2,1,0:T(1,128)} %reshape.619), calls=%async_computation.2 | async-start | bytes 32768 | tf_op jit(solution)/shard_map/all_to_all | solution.py:58
  152.9 5.1 collective-permute-start.25
  175.5 7.4 all-to-all-start
  189.7 7.7 all-to-all-start.3
  205.7 7.8 all-to-all-start.1
  236.6 5.8 collective-permute-start.35
  244.4 5.8 collective-permute-start.39
  262.4 5.8 collective-permute-start.43
  270.0 5.7 collective-permute-start.46
  286.5 12.2 %all_to_all.50 = f32[32,1,128]{2,1,0:T(1,128)S(1)} all-to-all(f32[32,1,128]{2,1,0:T(1,128)S(1)} %reshape.621), channel_id=1, replica_groups=mesh['gx'=8,'gy'=32] {'gy'}, dimensions={0} | all-to-all | bytes 32768 | tf_op jit(solution)/shard_map/all_to_all | solution.py:58
  300.3 7.7 all-to-all-start.5
  332.8 5.8 collective-permute-start.51
  351.4 5.8 collective-permute-start.55
  359.1 5.8 collective-permute-start.59
  377.2 5.8 collective-permute-start.63
  385.0 5.8 collective-permute-start.66
  399.8 5.2 collective-permute-done.67
  433.9 12.4 %all_to_all.51 = f32[32,1,128]{2,1,0:T(1,128)S(1)} all-to-all(f32[32,1,128]{2,1,0:T(1,128)S(1)} %reshape.623), channel_id=1, replica_groups=mesh['gx'=8,'gy'=32] {'gy'}, dimensions={0} | all-to-all | bytes 32768 | tf_op jit(solution)/shard_map/all_to_all | solution.py:58
  447.3 13.3 %all_to_all.52 = f32[8,8,512]{2,1,0:T(8,128)S(1)} all-to-all(f32[8,8,512]{2,1,0:T(8,128)S(1)} %broadcast_in_dim.135), channel_id=1, replica_groups=mesh['gx'=8,'gy'=32] {'gx'}, dimensions={0} | all-to-all | bytes 262144 | tf_op jit(solution)/shard_map/all_to_all | solution.py:58
  475.0 5.8 collective-permute-start.79
  499.3 5.8 collective-permute-start.83
  519.2 5.8 collective-permute-start.87
  527.0 5.8 collective-permute-start.91
  545.4 5.8 collective-permute-start.95
  560.7 5.3 collective-permute-start.98
  568.2 5.2 collective-permute-done.99
  587.8 5.2 collective-permute-done.103
  604.1 5.2 collective-permute-done.107
  638.2 12.4 %all_to_all.53 = f32[32,1,128]{2,1,0:T(1,128)S(1)} all-to-all(f32[32,1,128]{2,1,0:T(1,128)S(1)} %reshape.625), channel_id=1, replica_groups=mesh['gx'=8,'gy'=32] {'gy'}, dimensions={0} | all-to-all | bytes 32768 | tf_op jit(solution)/shard_map/all_to_all | solution.py:58
  651.6 13.3 %all_to_all.54 = f32[8,8,512]{2,1,0:T(8,128)S(1)} all-to-all(f32[8,8,512]{2,1,0:T(8,128)S(1)} %broadcast_in_dim.141), channel_id=1, replica_groups=mesh['gx'=8,'gy'=32] {'gx'}, dimensions={0} | all-to-all | bytes 262144 | tf_op jit(solution)/shard_map/all_to_all | solution.py:58
  679.3 5.8 collective-permute-start.119
  698.0 5.8 collective-permute-start.123
  723.6 5.8 collective-permute-start.127
  735.8 6.9 reshape.581
  753.5 5.8 collective-permute-start.131
  761.3 5.8 collective-permute-start.135
  776.8 5.2 collective-permute-start.138
  784.0 5.8 collective-permute-done.139
  (565 shorter events, 449.7 us)
Async XLA Ops:
  1.7 34.7 %collective-permute-start.2 = (f32[128,1]{1,0:T(8,128)S(1)}, f32[128,1]{1,0:T(8,128)S(1)}, u32[]{:S(2)}, u32[]{:S(2)}) collective-permute-start(f32[128,1]{1,0:T(8,128)S(1)} %get-tuple-element.62), channel_id=1, source_target_pairs={{1,0},{2,1},{3,2},{4,3},{5,4},{6,5},{7,6},{8,7},{9,8},{10,9},{11,1... | collective-permute-start | bytes 1544 | tf_op jit(solution)/shard_map/ppermute | solution.py:22
  5.7 30.7 %collective-permute-start.3 = (f32[128,1]{1,0:T(8,128)S(1)}, f32[128,1]{1,0:T(8,128)S(1)}, u32[]{:S(2)}, u32[]{:S(2)}) collective-permute-start(f32[128,1]{1,0:T(8,128)S(1)} %get-tuple-element.63), channel_id=1, source_target_pairs={{0,1},{1,2},{2,3},{3,4},{4,5},{5,6},{6,7},{7,8},{8,9},{9,10},{10,1... | collective-permute-start | bytes 1544 | tf_op jit(solution)/shard_map/ppermute | solution.py:21
  7.6 28.8 %collective-permute-start = (f32[1,256]{1,0:T(1,128)S(1)}, f32[1,256]{1,0:T(1,128)S(1)}, u32[]{:S(2)}, u32[]{:S(2)}) collective-permute-start(f32[1,256]{1,0:T(1,128)S(1)} %get-tuple-element.65), channel_id=1, source_target_pairs={{32,0},{64,32},{96,64},{128,96},{160,128},{192,160},{224,192},{33,... | collective-permute-start | bytes 3080 | tf_op jit(solution)/shard_map/ppermute | solution.py:22
  9.7 26.7 %collective-permute-start.1 = (f32[1,256]{1,0:T(1,128)S(1)}, f32[1,256]{1,0:T(1,128)S(1)}, u32[]{:S(2)}, u32[]{:S(2)}) collective-permute-start(f32[1,256]{1,0:T(1,128)S(1)} %get-tuple-element.64), channel_id=1, source_target_pairs={{0,32},{32,64},{64,96},{96,128},{128,160},{160,192},{192,224},{1,3... | collective-permute-start | bytes 3080 | tf_op jit(solution)/shard_map/ppermute | solution.py:21
  36.7 16.5 %collective-permute-start.6 = (f32[128,1]{1,0:T(8,128)S(1)}, f32[128,1]{1,0:T(8,128)S(1)}, u32[]{:S(2)}, u32[]{:S(2)}) collective-permute-start(f32[128,1]{1,0:T(8,128)S(1)} %get-tuple-element.58), channel_id=1, source_target_pairs={{1,0},{2,1},{3,2},{4,3},{5,4},{6,5},{7,6},{8,7},{9,8},{10,9},{11,1... | collective-permute-start | bytes 1544 | tf_op jit(solution)/shard_map/ppermute | solution.py:22
  71.9 14.6 %collective-permute-start.10 = (f32[64,1]{1,0:T(8,128)S(1)}, f32[64,1]{1,0:T(8,128)S(1)}, u32[]{:S(2)}, u32[]{:S(2)}) collective-permute-start(f32[64,1]{1,0:T(8,128)S(1)} %get-tuple-element.105), channel_id=1, source_target_pairs={{1,0},{2,1},{3,2},{4,3},{5,4},{6,5},{7,6},{8,7},{9,8},{10,9},{11,1... | collective-permute-start | bytes 776 | tf_op jit(solution)/shard_map/ppermute | solution.py:22
  87.5 14.0 %collective-permute-start.14 = (f32[64,1]{1,0:T(8,128)S(1)}, f32[64,1]{1,0:T(8,128)S(1)}, u32[]{:S(2)}, u32[]{:S(2)}) collective-permute-start(f32[64,1]{1,0:T(8,128)S(1)} %get-tuple-element.101), channel_id=1, source_target_pairs={{1,0},{2,1},{3,2},{4,3},{5,4},{6,5},{7,6},{8,7},{9,8},{10,9},{11,1... | collective-permute-start | bytes 776 | tf_op jit(solution)/shard_map/ppermute | solution.py:22
  105.9 14.6 %collective-permute-start.18 = (f32[32,1]{1,0:T(8,128)S(1)}, f32[32,1]{1,0:T(8,128)S(1)}, u32[]{:S(2)}, u32[]{:S(2)}) collective-permute-start(f32[32,1]{1,0:T(8,128)S(1)} %get-tuple-element.156), channel_id=1, source_target_pairs={{1,0},{2,1},{3,2},{4,3},{5,4},{6,5},{7,6},{8,7},{9,8},{10,9},{11,1... | collective-permute-start | bytes 392 | tf_op jit(solution)/shard_map/ppermute | solution.py:22
  121.2 22.4 %collective-permute-start.22 = (f32[32,1]{1,0:T(8,128)S(1)}, f32[32,1]{1,0:T(8,128)S(1)}, u32[]{:S(2)}, u32[]{:S(2)}) collective-permute-start(f32[32,1]{1,0:T(8,128)S(1)} %get-tuple-element.152), channel_id=1, source_target_pairs={{1,0},{2,1},{3,2},{4,3},{5,4},{6,5},{7,6},{8,7},{9,8},{10,9},{11,1... | collective-permute-start | bytes 392 | tf_op jit(solution)/shard_map/ppermute | solution.py:22
  126.1 17.5 %collective-permute-start.20 = (f32[1,64]{1,0:T(1,128)S(1)}, f32[1,64]{1,0:T(1,128)S(1)}, u32[]{:S(2)}, u32[]{:S(2)}) collective-permute-start(f32[1,64]{1,0:T(1,128)S(1)} %get-tuple-element.155), channel_id=1, source_target_pairs={{32,0},{64,32},{96,64},{128,96},{160,128},{192,160},{224,192},{33,... | collective-permute-start | bytes 776 | tf_op jit(solution)/shard_map/ppermute | solution.py:22
  128.1 15.6 %collective-permute-start.21 = (f32[1,64]{1,0:T(1,128)S(1)}, f32[1,64]{1,0:T(1,128)S(1)}, u32[]{:S(2)}, u32[]{:S(2)}) collective-permute-start(f32[1,64]{1,0:T(1,128)S(1)} %get-tuple-element.154), channel_id=1, source_target_pairs={{0,32},{32,64},{64,96},{96,128},{128,160},{160,192},{192,224},{1,3... | collective-permute-start | bytes 776 | tf_op jit(solution)/shard_map/ppermute | solution.py:21
  135.1 40.4 %all-to-all-start.2 = ((f32[32,1,128]{2,1,0:T(1,128)}), f32[32,1,128]{2,1,0:T(1,128)S(1)}, u32[]{:S(2)}, u32[]{:S(2)}) async-start(f32[32,1,128]{2,1,0:T(1,128)} %reshape.619), calls=%async_computation.2 | async-start | bytes 32768 | tf_op jit(solution)/shard_map/all_to_all | solution.py:58
  144.8 13.3 %collective-permute-start.26 = (f32[16,1]{1,0:T(8,128)S(1)}, f32[16,1]{1,0:T(8,128)S(1)}, u32[]{:S(2)}, u32[]{:S(2)}) collective-permute-start(f32[16,1]{1,0:T(8,128)S(1)} %get-tuple-element.191), channel_id=1, source_target_pairs={{1,0},{2,1},{3,2},{4,3},{5,4},{6,5},{7,6},{8,7},{9,8},{10,9},{11,1... | collective-permute-start | bytes 200 | tf_op jit(solution)/shard_map/ppermute | solution.py:22
  159.5 13.6 %collective-permute-start.30 = (f32[16,1]{1,0:T(8,128)S(1)}, f32[16,1]{1,0:T(8,128)S(1)}, u32[]{:S(2)}, u32[]{:S(2)}) collective-permute-start(f32[16,1]{1,0:T(8,128)S(1)} %get-tuple-element.187), channel_id=1, source_target_pairs={{1,0},{2,1},{3,2},{4,3},{5,4},{6,5},{7,6},{8,7},{9,8},{10,9},{11,1... | collective-permute-start | bytes 200 | tf_op jit(solution)/shard_map/ppermute | solution.py:22
  175.5 13.5 %all-to-all-start = ((f32[32,1,128]{2,1,0:T(1,128)}), f32[32,1,128]{2,1,0:T(1,128)S(1)}, u32[]{:S(2)}, u32[]{:S(2)}) async-start(f32[32,1,128]{2,1,0:T(1,128)} %reshape.617), calls=%async_computation | async-start | bytes 32768 | tf_op jit(solution)/shard_map/all_to_all | solution.py:58
  189.7 15.3 %all-to-all-start.3 = ((f32[8,8,512]{2,1,0:T(8,128)}), f32[8,8,512]{2,1,0:T(8,128)S(1)}, u32[]{:S(2)}, u32[]{:S(2)}) async-start(f32[8,8,512]{2,1,0:T(8,128)} %broadcast_in_dim.126), calls=%async_computation.3 | async-start | bytes 262144 | tf_op jit(solution)/shard_map/all_to_all | solution.py:58
  197.5 33.7 %collective-permute-start.36 = (f32[2,32]{1,0:T(2,128)S(1)}, f32[2,32]{1,0:T(2,128)S(1)}, u32[]{:S(2)}, u32[]{:S(2)}) collective-permute-start(f32[2,32]{1,0:T(2,128)S(1)} %get-tuple-element.18), channel_id=1, source_target_pairs={{0,32},{32,64},{64,96},{96,128},{128,160},{160,192},{192,224},{1,3... | collective-permute-start | bytes 776 | tf_op jit(solution)/shard_map/ppermute | solution.py:41
  202.1 29.1 %collective-permute-start.37 = (f32[2,32]{1,0:T(2,128)S(1)}, f32[2,32]{1,0:T(2,128)S(1)}, u32[]{:S(2)}, u32[]{:S(2)}) collective-permute-start(f32[2,32]{1,0:T(2,128)S(1)} %get-tuple-element.19), channel_id=1, source_target_pairs={{32,0},{64,32},{96,64},{128,96},{160,128},{192,160},{224,192},{33,... | collective-permute-start | bytes 776 | tf_op jit(solution)/shard_map/ppermute | solution.py:43
  205.7 13.5 %all-to-all-start.1 = ((f32[8,8,512]{2,1,0:T(8,128)}), f32[8,8,512]{2,1,0:T(8,128)S(1)}, u32[]{:S(2)}, u32[]{:S(2)}) async-start(f32[8,8,512]{2,1,0:T(8,128)} %broadcast_in_dim.124), calls=%async_computation.1 | async-start | bytes 262144 | tf_op jit(solution)/shard_map/all_to_all | solution.py:58
  234.7 15.4 %collective-permute-start.34 = (f32[2,20,2]{2,1,0:T(8,128)S(1)}, f32[2,20,2]{2,1,0:T(8,128)S(1)}, u32[]{:S(2)}, u32[]{:S(2)}) collective-permute-start(f32[2,20,2]{2,1,0:T(8,128)S(1)} %get-tuple-element.127), channel_id=1, source_target_pairs={{0,1},{1,2},{2,3},{3,4},{4,5},{5,6},{6,7},{7,8},{8,9},{9,10},{10,1... | collective-permute-start | bytes 968 | tf_op jit(solution)/shard_map/ppermute | solution.py:41
  236.6 13.5 %collective-permute-start.35 = (f32[2,20,2]{2,1,0:T(8,128)S(1)}, f32[2,20,2]{2,1,0:T(8,128)S(1)}, u32[]{:S(2)}, u32[]{:S(2)}) collective-permute-start(f32[2,20,2]{2,1,0:T(8,128)S(1)} %get-tuple-element.128), channel_id=1, source_target_pairs={{1,0},{2,1},{3,2},{4,3},{5,4},{6,5},{7,6},{8,7},{9,8},{10,9},{11,1... | collective-permute-start | bytes 968 | tf_op jit(solution)/shard_map/ppermute | solution.py:43
  270.0 14.8 %collective-permute-start.46 = (f32[16,1]{1,0:T(8,128)S(1)}, f32[16,1]{1,0:T(8,128)S(1)}, u32[]{:S(2)}, u32[]{:S(2)}) collective-permute-start(f32[16,1]{1,0:T(8,128)S(1)} %get-tuple-element.180), channel_id=1, source_target_pairs={{1,0},{2,1},{3,2},{4,3},{5,4},{6,5},{7,6},{8,7},{9,8},{10,9},{11,1... | collective-permute-start | bytes 200 | tf_op jit(solution)/shard_map/ppermute | solution.py:22
  300.3 15.4 %all-to-all-start.5 = ((f32[8,8,512]{2,1,0:T(8,128)}), f32[8,8,512]{2,1,0:T(8,128)S(1)}, u32[]{:S(2)}, u32[]{:S(2)}) async-start(f32[8,8,512]{2,1,0:T(8,128)} %broadcast_in_dim.130), calls=%async_computation.5 | async-start | bytes 262144 | tf_op jit(solution)/shard_map/all_to_all | solution.py:58
  309.0 37.6 %collective-permute-start.56 = (f32[2,64]{1,0:T(2,128)S(1)}, f32[2,64]{1,0:T(2,128)S(1)}, u32[]{:S(2)}, u32[]{:S(2)}) collective-permute-start(f32[2,64]{1,0:T(2,128)S(1)} %get-tuple-element.10), channel_id=1, source_target_pairs={{0,32},{32,64},{64,96},{96,128},{128,160},{160,192},{192,224},{1,3... | collective-permute-start | bytes 1544 | tf_op jit(solution)/shard_map/ppermute | solution.py:41
  313.6 33.0 %collective-permute-start.57 = (f32[2,64]{1,0:T(2,128)S(1)}, f32[2,64]{1,0:T(2,128)S(1)}, u32[]{:S(2)}, u32[]{:S(2)}) collective-permute-start(f32[2,64]{1,0:T(2,128)S(1)} %get-tuple-element.11), channel_id=1, source_target_pairs={{32,0},{64,32},{96,64},{128,96},{160,128},{192,160},{224,192},{33,... | collective-permute-start | bytes 1544 | tf_op jit(solution)/shard_map/ppermute | solution.py:43
  349.5 15.4 %collective-permute-start.54 = (f32[2,36,2]{2,1,0:T(8,128)S(1)}, f32[2,36,2]{2,1,0:T(8,128)S(1)}, u32[]{:S(2)}, u32[]{:S(2)}) collective-permute-start(f32[2,36,2]{2,1,0:T(8,128)S(1)} %get-tuple-element.86), channel_id=1, source_target_pairs={{0,1},{1,2},{2,3},{3,4},{4,5},{5,6},{6,7},{7,8},{8,9},{9,10},{10,1... | collective-permute-start | bytes 1736 | tf_op jit(solution)/shard_map/ppermute | solution.py:41
  351.4 13.5 %collective-permute-start.55 = (f32[2,36,2]{2,1,0:T(8,128)S(1)}, f32[2,36,2]{2,1,0:T(8,128)S(1)}, u32[]{:S(2)}, u32[]{:S(2)}) collective-permute-start(f32[2,36,2]{2,1,0:T(8,128)S(1)} %get-tuple-element.87), channel_id=1, source_target_pairs={{1,0},{2,1},{3,2},{4,3},{5,4},{6,5},{7,6},{8,7},{9,8},{10,9},{11,1... | collective-permute-start | bytes 1736 | tf_op jit(solution)/shard_map/ppermute | solution.py:43
  385.0 14.8 %collective-permute-start.66 = (f32[32,1]{1,0:T(8,128)S(1)}, f32[32,1]{1,0:T(8,128)S(1)}, u32[]{:S(2)}, u32[]{:S(2)}) collective-permute-start(f32[32,1]{1,0:T(8,128)S(1)} %get-tuple-element.145), channel_id=1, source_target_pairs={{1,0},{2,1},{3,2},{4,3},{5,4},{6,5},{7,6},{8,7},{9,8},{10,9},{11,1... | collective-permute-start | bytes 392 | tf_op jit(solution)/shard_map/ppermute | solution.py:22
  390.8 14.2 %collective-permute-start.64 = (f32[1,64]{1,0:T(1,128)S(1)}, f32[1,64]{1,0:T(1,128)S(1)}, u32[]{:S(2)}, u32[]{:S(2)}) collective-permute-start(f32[1,64]{1,0:T(1,128)S(1)} %get-tuple-element.148), channel_id=1, source_target_pairs={{32,0},{64,32},{96,64},{128,96},{160,128},{192,160},{224,192},{33,... | collective-permute-start | bytes 776 | tf_op jit(solution)/shard_map/ppermute | solution.py:22
  419.0 13.1 %collective-permute-start.74 = (f32[16,1]{1,0:T(8,128)S(1)}, f32[16,1]{1,0:T(8,128)S(1)}, u32[]{:S(2)}, u32[]{:S(2)}) collective-permute-start(f32[16,1]{1,0:T(8,128)S(1)} %get-tuple-element.170), channel_id=1, source_target_pairs={{1,0},{2,1},{3,2},{4,3},{5,4},{6,5},{7,6},{8,7},{9,8},{10,9},{11,1... | collective-permute-start | bytes 200 | tf_op jit(solution)/shard_map/ppermute | solution.py:22
  473.1 13.5 %collective-permute-start.78 = (f32[2,20,2]{2,1,0:T(8,128)S(1)}, f32[2,20,2]{2,1,0:T(8,128)S(1)}, u32[]{:S(2)}, u32[]{:S(2)}) collective-permute-start(f32[2,20,2]{2,1,0:T(8,128)S(1)} %get-tuple-element.115), channel_id=1, source_target_pairs={{0,1},{1,2},{2,3},{3,4},{4,5},{5,6},{6,7},{7,8},{8,9},{9,10},{10,1... | collective-permute-start | bytes 968 | tf_op jit(solution)/shard_map/ppermute | solution.py:41
  480.8 33.7 %collective-permute-start.88 = (f32[2,128]{1,0:T(2,128)S(1)}, f32[2,128]{1,0:T(2,128)S(1)}, u32[]{:S(2)}, u32[]{:S(2)}) collective-permute-start(f32[2,128]{1,0:T(2,128)S(1)} %get-tuple-element.2), channel_id=1, source_target_pairs={{0,32},{32,64},{64,96},{96,128},{128,160},{160,192},{192,224},{1,3... | collective-permute-start | bytes 3080 | tf_op jit(solution)/shard_map/ppermute | solution.py:41
  482.8 31.7 %collective-permute-start.89 = (f32[2,128]{1,0:T(2,128)S(1)}, f32[2,128]{1,0:T(2,128)S(1)}, u32[]{:S(2)}, u32[]{:S(2)}) collective-permute-start(f32[2,128]{1,0:T(2,128)S(1)} %get-tuple-element.3), channel_id=1, source_target_pairs={{32,0},{64,32},{96,64},{128,96},{160,128},{192,160},{224,192},{33,... | collective-permute-start | bytes 3080 | tf_op jit(solution)/shard_map/ppermute | solution.py:43
  517.3 15.4 %collective-permute-start.86 = (f32[2,68,2]{2,1,0:T(8,128)S(1)}, f32[2,68,2]{2,1,0:T(8,128)S(1)}, u32[]{:S(2)}, u32[]{:S(2)}) collective-permute-start(f32[2,68,2]{2,1,0:T(8,128)S(1)} %get-tuple-element.70), channel_id=1, source_target_pairs={{0,1},{1,2},{2,3},{3,4},{4,5},{5,6},{6,7},{7,8},{8,9},{9,10},{10,1... | collective-permute-start | bytes 3272 | tf_op jit(solution)/shard_map/ppermute | solution.py:41
  519.2 13.5 %collective-permute-start.87 = (f32[2,68,2]{2,1,0:T(8,128)S(1)}, f32[2,68,2]{2,1,0:T(8,128)S(1)}, u32[]{:S(2)}, u32[]{:S(2)}) collective-permute-start(f32[2,68,2]{2,1,0:T(8,128)S(1)} %get-tuple-element.71), channel_id=1, source_target_pairs={{1,0},{2,1},{3,2},{4,3},{5,4},{6,5},{7,6},{8,7},{9,8},{10,9},{11,1... | collective-permute-start | bytes 3272 | tf_op jit(solution)/shard_map/ppermute | solution.py:43
  553.7 19.7 %collective-permute-start.96 = (f32[1,128]{1,0:T(1,128)S(1)}, f32[1,128]{1,0:T(1,128)S(1)}, u32[]{:S(2)}, u32[]{:S(2)}) collective-permute-start(f32[1,128]{1,0:T(1,128)S(1)} %get-tuple-element.97), channel_id=1, source_target_pairs={{32,0},{64,32},{96,64},{128,96},{160,128},{192,160},{224,192},{33,... | collective-permute-start | bytes 1544 | tf_op jit(solution)/shard_map/ppermute | solution.py:22
  556.4 17.0 %collective-permute-start.97 = (f32[1,128]{1,0:T(1,128)S(1)}, f32[1,128]{1,0:T(1,128)S(1)}, u32[]{:S(2)}, u32[]{:S(2)}) collective-permute-start(f32[1,128]{1,0:T(1,128)S(1)} %get-tuple-element.96), channel_id=1, source_target_pairs={{0,32},{32,64},{64,96},{96,128},{128,160},{160,192},{192,224},{1,3... | collective-permute-start | bytes 1544 | tf_op jit(solution)/shard_map/ppermute | solution.py:21
  578.8 14.2 %collective-permute-start.100 = (f32[1,64]{1,0:T(1,128)S(1)}, f32[1,64]{1,0:T(1,128)S(1)}, u32[]{:S(2)}, u32[]{:S(2)}) collective-permute-start(f32[1,64]{1,0:T(1,128)S(1)} %get-tuple-element.140), channel_id=1, source_target_pairs={{32,0},{64,32},{96,64},{128,96},{160,128},{192,160},{224,192},{33,... | collective-permute-start | bytes 776 | tf_op jit(solution)/shard_map/ppermute | solution.py:22
  595.1 14.2 %collective-permute-start.104 = (f32[1,64]{1,0:T(1,128)S(1)}, f32[1,64]{1,0:T(1,128)S(1)}, u32[]{:S(2)}, u32[]{:S(2)}) collective-permute-start(f32[1,64]{1,0:T(1,128)S(1)} %get-tuple-element.136), channel_id=1, source_target_pairs={{32,0},{64,32},{96,64},{128,96},{160,128},{192,160},{224,192},{33,... | collective-permute-start | bytes 776 | tf_op jit(solution)/shard_map/ppermute | solution.py:22
  597.0 12.3 %collective-permute-start.105 = (f32[1,64]{1,0:T(1,128)S(1)}, f32[1,64]{1,0:T(1,128)S(1)}, u32[]{:S(2)}, u32[]{:S(2)}) collective-permute-start(f32[1,64]{1,0:T(1,128)S(1)} %get-tuple-element.135), channel_id=1, source_target_pairs={{0,32},{32,64},{64,96},{96,128},{128,160},{160,192},{192,224},{1,3... | collective-permute-start | bytes 776 | tf_op jit(solution)/shard_map/ppermute | solution.py:21
  623.3 13.1 %collective-permute-start.114 = (f32[16,1]{1,0:T(8,128)S(1)}, f32[16,1]{1,0:T(8,128)S(1)}, u32[]{:S(2)}, u32[]{:S(2)}) collective-permute-start(f32[16,1]{1,0:T(8,128)S(1)} %get-tuple-element.162), channel_id=1, source_target_pairs={{1,0},{2,1},{3,2},{4,3},{5,4},{6,5},{7,6},{8,7},{9,8},{10,9},{11,1... | collective-permute-start | bytes 200 | tf_op jit(solution)/shard_map/ppermute | solution.py:22
  696.1 13.6 %collective-permute-start.122 = (f32[2,36,2]{2,1,0:T(8,128)S(1)}, f32[2,36,2]{2,1,0:T(8,128)S(1)}, u32[]{:S(2)}, u32[]{:S(2)}) collective-permute-start(f32[2,36,2]{2,1,0:T(8,128)S(1)} %get-tuple-element.74), channel_id=1, source_target_pairs={{0,1},{1,2},{2,3},{3,4},{4,5},{5,6},{6,7},{7,8},{8,9},{9,10},{10,1... | collective-permute-start | bytes 1736 | tf_op jit(solution)/shard_map/ppermute | solution.py:41
  703.8 44.9 %collective-permute-start.132 = (f32[2,256]{1,0:T(2,128)S(1)}, f32[2,256]{1,0:T(2,128)S(1)}, u32[]{:S(2)}, u32[]{:S(2)}) collective-permute-start(f32[2,256]{1,0:T(2,128)S(1)} %get-tuple-element.54), channel_id=1, source_target_pairs={{0,32},{32,64},{64,96},{96,128},{128,160},{160,192},{192,224},{1,3... | collective-permute-start | bytes 6152 | tf_op jit(solution)/shard_map/ppermute | solution.py:41
  705.9 42.7 %collective-permute-start.133 = (f32[2,256]{1,0:T(2,128)S(1)}, f32[2,256]{1,0:T(2,128)S(1)}, u32[]{:S(2)}, u32[]{:S(2)}) collective-permute-start(f32[2,256]{1,0:T(2,128)S(1)} %get-tuple-element.55), channel_id=1, source_target_pairs={{32,0},{64,32},{96,64},{128,96},{160,128},{192,160},{224,192},{33,... | collective-permute-start | bytes 6152 | tf_op jit(solution)/shard_map/ppermute | solution.py:43
  751.6 15.5 %collective-permute-start.130 = (f32[2,132,2]{2,1,0:T(8,128)S(1)}, f32[2,132,2]{2,1,0:T(8,128)S(1)}, u32[]{:S(2)}, u32[]{:S(2)}) collective-permute-start(f32[2,132,2]{2,1,0:T(8,128)S(1)} %get-tuple-element.38), channel_id=1, source_target_pairs={{0,1},{1,2},{2,3},{3,4},{4,5},{5,6},{6,7},{7,8},{8,9},{9,10},{10,1... | collective-permute-start | bytes 6344 | tf_op jit(solution)/shard_map/ppermute | solution.py:41
  753.5 13.5 %collective-permute-start.131 = (f32[2,132,2]{2,1,0:T(8,128)S(1)}, f32[2,132,2]{2,1,0:T(8,128)S(1)}, u32[]{:S(2)}, u32[]{:S(2)}) collective-permute-start(f32[2,132,2]{2,1,0:T(8,128)S(1)} %get-tuple-element.39), channel_id=1, source_target_pairs={{1,0},{2,1},{3,2},{4,3},{5,4},{6,5},{7,6},{8,7},{9,8},{10,9},{11,1... | collective-permute-start | bytes 6344 | tf_op jit(solution)/shard_map/ppermute | solution.py:43
  769.7 20.1 %collective-permute-start.136 = (f32[1,256]{1,0:T(1,128)S(1)}, f32[1,256]{1,0:T(1,128)S(1)}, u32[]{:S(2)}, u32[]{:S(2)}) collective-permute-start(f32[1,256]{1,0:T(1,128)S(1)} %get-tuple-element.53), channel_id=1, source_target_pairs={{32,0},{64,32},{96,64},{128,96},{160,128},{192,160},{224,192},{33,... | collective-permute-start | bytes 3080 | tf_op jit(solution)/shard_map/ppermute | solution.py:22
  772.4 17.4 %collective-permute-start.137 = (f32[1,256]{1,0:T(1,128)S(1)}, f32[1,256]{1,0:T(1,128)S(1)}, u32[]{:S(2)}, u32[]{:S(2)}) collective-permute-start(f32[1,256]{1,0:T(1,128)S(1)} %get-tuple-element.52), channel_id=1, source_target_pairs={{0,32},{32,64},{64,96},{96,128},{128,160},{160,192},{192,224},{1,3... | collective-permute-start | bytes 3080 | tf_op jit(solution)/shard_map/ppermute | solution.py:21
  (100 other events, 785.4 us)
where the time goes:
time: 803 us; the launch traced here: 791 us
  starting transfers between devices  510 us (64%)
  waiting for transfers between devices  106 us (13%)
  blocking collectives  63.6 us (8%)
  local copies, waits for them, and re-layouts  55.7 us (7%)
  other arithmetic  44.9 us (6%)
  between operations  11.1 us (1%)
    ppermute x34, starting transfers between devices, padded_2(): lax.ppermute(head, axis, [((i + 1) % count, i) for i in range(ends)])  154 us
    ppermute x36, starting transfers between devices, extended(): lax.ppermute(last, axis, up)  125 us
    ppermute x36, starting transfers between devices, extended(): lax.ppermute(first, axis, [(b, a) for a, b in up])  114 us
    ppermute x34, starting transfers between devices, padded_2(): lax.ppermute(tail, axis, [(i, (i + 1) % count) for i in range(ends)])  78.6 us
    all_to_all x5, blocking collectives, sent_to_all(): return lax.all_to_all(copies, axis, split_axis=0, concat_axis=0, tiled=True)  63.6 us
    ppermute x34, waiting for transfers between devices, padded_2(): lax.ppermute(head, axis, [((i + 1) % count, i) for i in range(ends)])  58.1 us
    all_to_all x5, starting transfers between devices, sent_to_all(): return lax.all_to_all(copies, axis, split_axis=0, concat_axis=0, tiled=True)  39.1 us
    ppermute x36, waiting for transfers between devices, extended(): lax.ppermute(last, axis, up)  37.6 us
  transfers between devices with their start and end apart: 145, of which 43 were waited for; matrix products, arithmetic and copies ran while one was open for 7% of the time, Pallas kernels for 0%

commit v1 on v0

v1 whole, which is shorter than its diff:
```python
import jax
import jax.numpy as jnp
from jax import lax
from jax.experimental import pallas as pl
from jax.experimental.pallas import tpu as pltpu
from jax.sharding import PartitionSpec as P

MESH = pl.DeviceIdType.MESH
F32 = jnp.float32
BF16 = jnp.bfloat16
GX, GY = 8, 32
NX, NY = 1024, 8192
LV_Q = [4.0 ** (-l) for l in range(5)]
LV_D = [4.0 ** (1 - l) for l in range(5)]

AROUND = [(-1, 0), (1, 0), (0, -1), (0, 1), (-1, -1), (-1, 1), (1, -1), (1, 1)]
SIDE = [-1, 1, -2, 2]
LINE = [-1, 1, -2, 2, -3, 3]
GROUP_A = [(dz, dc) for dz in range(8) for dc in range(2) if dz or dc]
GROUP_B = [(dy, dx) for dy in range(4) for dx in range(4) if dy or dx]


def iota(shape, dim):
    return lax.broadcasted_iota(jnp.int32, shape, dim)


def beside(v):
    r, c = v.shape
    return (
        pltpu.roll(v, 1, axis=0)
        + pltpu.roll(v, r - 1, axis=0)
        + pltpu.roll(v, 1, axis=1)
        + pltpu.roll(v, c - 1, axis=1)
    )


def inside(shape, level, row0, col0):
    rows = iota(shape, 0) + row0
    cols = iota(shape, 1) + col0
    return (
        (rows >= 0) & (rows < (NX >> level)) & (cols >= 0) & (cols < (NY >> level))
    )


class Level:
    def __init__(self, level, shift, row0, col0, mask=None):
        self.level = level
        self.d = LV_D[level] + shift
        ok = inside(shift.shape, level, row0, col0)
        if mask is not None:
            ok = ok & mask
        self.ok = ok
        self.k = jnp.where(ok, 0.8 / self.d, 0.0)
        self.km = self.k * LV_Q[level]

    def cut(self, lo, hi):
        out = object.__new__(Level)
        out.level = self.level
        out.d, out.k, out.km, out.ok = (
            self.d[lo:hi],
            self.k[lo:hi],
            self.km[lo:hi],
            None,
        )
        return out

    def sweep0(self, v):
        return 0.2 * v + self.km * beside(v)

    def sweep(self, v, kg):
        return 0.2 * v + kg + self.km * beside(v)

    def residual(self, v, g):
        return g - self.d * v + LV_Q[self.level] * beside(v)

    def apply(self, v):
        return self.d * v - LV_Q[self.level] * beside(v)


def mm(x, w):
    m = x.shape[0]
    a = x.astype(BF16)
    r = x - a.astype(F32)
    b = r.astype(BF16)
    c = (r - b.astype(F32)).astype(BF16)
    y = jnp.dot(jnp.concatenate([a, b, c], axis=0), w, preferred_element_type=F32)
    return (y[2 * m :] + y[m : 2 * m]) + y[:m]


def total(x):
    return jnp.sum(jnp.sum(x, axis=0, keepdims=True), axis=1, keepdims=True)


def pick(row, at):
    lane = iota(row.shape, 1)
    return jnp.sum(jnp.where(lane == at, row, 0.0), axis=1, keepdims=True)


def kernel(
    rhs, shf, sol, res,
    xg, xs, kk, kg0, v0, wa, wb, tmp0,
    t1, t2, t3,
    rm, r23, r34, p43, p32, p21, r03,
    s_side, s_line, g_side, g_line, own3, own3g, ownb,
    x2s, x2g, x2h, own2s, own2g, own2h,
    x3a, x3b, own3a, own3b,
    ar_in, ar_a, ar_b,
    e0_ss, e0_rs, s_ss, s_rs, g_ss, g_rs, x2_ss, x2_rs, x3_ss, x3_rs, ar_ss, ar_rs,
):
    gx = lax.axis_index("gx")
    gy = lax.axis_index("gy")
    core = lax.rem(gy, 2)
    quad = lax.div(gy, 2)
    qy, qx = lax.div(quad, 4), lax.rem(quad, 4)

    def near(dz, dy):
        return (lax.rem(gx + (dz + GX), GX), lax.rem(gy + (dy + GY), GY))

    def in_a(dz, dc):
        return (lax.rem(gx + dz, GX), gy - core + lax.rem(core + dc, 2))

    def in_b(dy, dx):
        return (gx, (lax.rem(qy + dy, 4) * 4 + lax.rem(qx + dx, 4)) * 2 + core)

    barrier = pltpu.get_barrier_semaphore()
    partners = (
        [near(*o) for o in AROUND]
        + [in_a(*o) for o in GROUP_A]
        + [in_b(*o) for o in GROUP_B]
    )
    for p in partners:
        pl.semaphore_signal(barrier, inc=1, device_id=p, device_id_type=MESH)

    sent = []

    def send(src, dst, ss, rs, dev):
        cp = pltpu.make_async_remote_copy(
            src_ref=src, dst_ref=dst, send_sem=ss, recv_sem=rs,
            device_id=dev, device_id_type=MESH,
        )
        cp.start()
        sent.append(cp)
        return cp

    i, j = iota((256, 128), 0), iota((256, 128), 1)
    rm[...] = jnp.where((i >> 1) == j, 0.25, 0.0).astype(BF16)
    r03[...] = jnp.where((i >> 3) + 48 == j, 1.0 / 64, 0.0).astype(BF16)
    i, j = iota((128, 128), 0), iota((128, 128), 1)
    r34[...] = jnp.where((i >> 1) == j, 0.25, 0.0).astype(BF16)
    r23[...] = jnp.where((i >> 1) + 32 == j, 0.25, 0.0).astype(BF16)
    p43[...] = jnp.where(i == (j >> 1), 1.0, 0.0).astype(BF16)
    p32[...] = jnp.where(i == (j >> 1) + 32, 1.0, 0.0).astype(BF16)
    i, j = iota((128, 256), 0), iota((128, 256), 1)
    p21[...] = jnp.where(i == (j >> 1), 1.0, 0.0).astype(BF16)

    def pair_rows(ref, rows, lanes):
        return jnp.concatenate(
            [
                ref[t, pl.ds(0, rows // 2, 2), :] + ref[t, pl.ds(1, rows // 2, 2), :]
                for t in range(lanes // 128)
            ],
            axis=1,
        )

    def put(ref, x):
        for t in range(x.shape[1] // 128):
            ref[t, 0 : x.shape[0], :] = x[:, 128 * t : 128 * t + 128]

    def restrict(x, ref, w):
        put(ref, x)
        return mm(pair_rows(ref, x.shape[0], x.shape[1]), w[...])

    def prolong(e, ref, w):
        y = mm(e, w[...])
        m = y.shape[0]
        out = []
        for t in range(y.shape[1] // 128):
            yt = y[:, 128 * t : 128 * t + 128]
            ref[t, pl.ds(0, m, 2), :] = yt
            ref[t, pl.ds(1, m, 2), :] = yt
            out.append(ref[t, 0 : 2 * m, :])
        return jnp.concatenate(out, axis=1) if len(out) > 1 else out[0]

    s0 = shf[...]
    for t in range(2):
        tmp0[t, 0:128, :] = s0[:, 128 * t : 128 * t + 128]
    acc = pair_rows(tmp0, 128, 256)
    put(t1, acc)
    acc = pair_rows(t1, 64, 256)
    put(t2, acc)
    acc = pair_rows(t2, 32, 256)
    own3[...] = mm(acc, r03[...])
    put(t1, s0)
    s1own = mm(pair_rows(t1, 128, 256), rm[...])
    put(t2, s1own)
    s2own = mm(pair_rows(t2, 64, 128), r34[...])
    own2s[...] = pltpu.roll(s2own, 32, axis=1)

    pl.semaphore_wait(barrier, len(partners))

    ROWS = {-1: (0, 32, 160, 192), 1: (96, 128, 0, 32), 0: (0, 128, 32, 160)}
    COLS = {-1: (0, 128, 384, 512), 1: (128, 256, 0, 128), 0: (0, 256, 128, 384)}
    first = []

    def border(f):
        src, dst = (shf, xs) if f else (rhs, xg)
        for n, (dz, dy) in enumerate(AROUND):
            a, b, c, d = ROWS[dz]
            e, g, h, k = COLS[dy]
            first.append(
                send(
                    src.at[a:b, e:g], dst.at[8 + c : 8 + d, h:k],
                    e0_ss.at[f, n], e0_rs.at[f, n], near(dz, dy),
                )
            )

    def side_send(src, buf, ss, rs):
        return [
            send(src, buf.at[n], ss.at[n], rs.at[n], near(0, d))
            for n, d in enumerate(SIDE)
        ]

    def side_join(own, buf, cps):
        for cp in cps:
            cp.wait_recv()
        right1, left1, right2, left2 = (buf[n] for n in range(4))
        lane = iota((16, 128), 1)
        out = jnp.where(lane < 48, pltpu.roll(left1, 96, axis=1), own)
        out = jnp.where(lane < 16, pltpu.roll(left2, 64, axis=1), out)
        out = jnp.where(lane >= 80, pltpu.roll(right1, 32, axis=1), out)
        return jnp.where(lane >= 112, pltpu.roll(right2, 64, axis=1), out)

    def line_send(src, buf, ss, rs):
        return [
            send(
                src, buf.at[16 * (3 - d) : 16 * (4 - d)],
                ss.at[4 + n], rs.at[4 + n], near(d, 0),
            )
            for n, d in enumerate(LINE)
        ]

    SRC2 = {-1: (0, 16), 1: (16, 32), 0: (0, 32)}

    def send2(src, buf, k):
        cps = []
        for n, (dz, dy) in enumerate(AROUND):
            a, b = SRC2[dz]
            cps.append(
                send(
                    src.at[a:b], buf.at[n, 0 : b - a],
                    x2_ss.at[k, n], x2_rs.at[k, n], near(dz, dy),
                )
            )
        return cps

    def lanes3(left, mid, right, lo, hi, move):
        lane = iota(mid.shape, 1)
        out = jnp.where(lane < lo, pltpu.roll(left, 128 - move, axis=1), mid)
        return jnp.where(lane >= hi, pltpu.roll(right, move, axis=1), out)

    def join2(own, buf, cps):
        for cp in cps:
            cp.wait_recv()
        dn, up, rt, lf, dr, dl, ur, ul = range(8)
        return jnp.concatenate(
            [
                lanes3(buf[ul, 0:16], buf[up, 0:16], buf[ur, 0:16], 32, 96, 64),
                lanes3(buf[lf], own, buf[rt], 32, 96, 64),
                lanes3(buf[dl, 0:16], buf[dn, 0:16], buf[dr, 0:16], 32, 96, 64),
            ],
            axis=0,
        )

    SRC3 = {-1: (8, 32), 1: (0, 24), 0: (8, 24)}

    def send3(src, buf, k):
        cps = []
        for n, (dz, dy) in enumerate(AROUND):
            a, b = SRC3[dz]
            cps.append(
                send(
                    src.at[a:b], buf.at[n, 0 : b - a],
                    x3_ss.at[k, n], x3_rs.at[k, n], near(dz, dy),
                )
            )
        return cps

    def join3(own, buf, cps):
        for cp in cps:
            cp.wait_recv()
        dn, up, rt, lf, dr, dl, ur, ul = range(8)
        return jnp.concatenate(
            [
                lanes3(buf[ul], buf[up], buf[ur], 48, 80, 32),
                lanes3(buf[lf, 0:16], own, buf[rt, 0:16], 48, 80, 32),
                lanes3(buf[dl], buf[dn], buf[dr], 48, 80, 32),
            ],
            axis=0,
        )

    def sum_start(row, k):
        ar_in[k, 0] = row
        return [
            send(
                ar_in.at[k, 0], ar_a.at[k, n],
                ar_ss.at[k, 0, n], ar_rs.at[k, 0, n], in_a(*o),
            )
            for n, o in enumerate(GROUP_A)
        ]

    def sum_next(cps, k):
        for cp in cps:
            cp.wait_recv()
        part = ar_in[k, 0] + jnp.sum(ar_a[k], axis=0)
        ar_in[k, 1] = part
        return [
            send(
                ar_in.at[k, 1], ar_b.at[k, n],
                ar_ss.at[k, 1, n], ar_rs.at[k, 1, n], in_b(*o),
            )
            for n, o in enumerate(GROUP_B)
        ]

    def sum_end(cps, k):
        for cp in cps:
            cp.wait_recv()
        return ar_in[k, 1] + jnp.sum(ar_b[k], axis=0)

    side_s = side_send(own3, s_side, s_ss, s_rs)
    border(1)
    border(0)
    cps2s = send2(own2s, x2s, 0)
    xs[8 + 32 : 8 + 160, 128:384] = s0
    xg[8 + 32 : 8 + 160, 128:384] = rhs[...]
    zero8 = jnp.zeros((8, 512), F32)
    for ref in (kg0, v0, wa, wb):
        ref[0:8, :] = zero8
        ref[200:208, :] = zero8

    row0 = gx * 128 - 32
    col0 = gy * 256 - 128
    for cp in first[:8]:
        cp.wait_recv()
    STEP = 16

    def near4(ref, r, n=STEP):
        c = ref[8 + r : 8 + r + n, :]
        around = (
            ref[7 + r : 7 + r + n, :]
            + ref[9 + r : 9 + r + n, :]
            + pltpu.roll(c, 1, axis=1)
            + pltpu.roll(c, 511, axis=1)
        )
        return c, around

    for r in range(0, 192, STEP):
        w = slice(8 + r, 8 + r + STEP)
        ok = inside((STEP, 512), 0, row0 + r, col0)
        kk[w, :] = jnp.where(ok, 0.8 / (4.0 + xs[w, :]), 0.0)
    put(tmp0, xs[8:200, :])
    s1 = jnp.concatenate(
        [
            mm(tmp0_pair(tmp0, t, 192), rm[...])
            for t in range(2)
        ],
        axis=1,
    )
    l1 = Level(1, s1, gx * 64 - 16, gy * 128 - 64)
    s2 = restrict(s1, t1, rm)

    s_row = side_join(own3[...], s_side, side_s)
    ownb[0] = s_row
    line_s = line_send(ownb.at[0], s_line, s_ss, s_rs)
    s_line[48:64] = s_row

    for cp in first[8:]:
        cp.wait_recv()
    for r in range(0, 192, STEP):
        w = slice(8 + r, 8 + r + STEP)
        kg0[w, :] = kk[w, :] * xg[w, :]
    for r in range(0, 192, STEP):
        w = slice(8 + r, 8 + r + STEP)
        c, around = near4(kg0, r)
        v0[w, :] = 1.2 * c + kk[w, :] * around
    for r in range(0, 192, STEP):
        w = slice(8 + r, 8 + r + STEP)
        c, around = near4(v0, r)
        out = xg[w, :] - (4.0 + xs[w, :]) * c + around
        for t in range(4):
            tmp0[t, r : r + STEP, :] = out[:, 128 * t : 128 * t + 128]
    g1 = jnp.concatenate([mm(tmp0_pair(tmp0, t, 192), rm[...]) for t in range(2)], axis=1)

    kg1 = l1.k * g1
    v1 = l1.sweep(kg1, kg1)
    g2 = restrict(l1.residual(v1, g1), t1, rm)
    l2a = Level(2, s2, gx * 32 - 8, gy * 64 - 32)
    kg = l2a.k * g2
    r2 = l2a.residual(l2a.sweep(kg, kg), g2)
    own2g[...] = g2[8:40]
    g3 = restrict(r2, t2, r23)
    g3own = g3[4:20]
    own3g[...] = g3own
    side_g = side_send(own3g, g_side, g_ss, g_rs)
    cps2g = send2(own2g, x2g, 1)

    for cp in line_s:
        cp.wait_recv()
    l3 = Level(3, s_line[...], gx * 16 - 48, gy * 32 - 48)
    s4 = restrict(s_line[...], t3, r34)
    l4 = Level(4, s4, gx * 8 - 24, gy * 16 - 24, iota((56, 128), 1) < 64)

    g_row = side_join(g3own, g_side, side_g)
    ownb[1] = g_row
    line_g = line_send(ownb.at[1], g_line, g_ss, g_rs)
    g_line[48:64] = g_row

    one4 = jnp.where(l4.ok, 1.0, 0.0)
    one3 = jnp.where(l3.ok, 1.0, 0.0)
    w6 = one4
    for _ in range(6):
        w6 = l4.sweep0(w6)
    w12 = w6
    for _ in range(6):
        w12 = l4.sweep0(w12)
    y3 = l3.sweep0(l3.sweep0(one3))
    u = l3.sweep0(l3.sweep0(y3))
    q = 4.0 * restrict(jnp.where(l3.ok, l3.apply(u), 0.0), t3, r34)
    kq = l4.k * q
    z = kq
    for _ in range(11):
        z = l4.sweep(z, kq)
    f3 = l3.sweep0(l3.sweep0(u - 0.25 * prolong(z, t3, p43)))
    f2 = l3.sweep0(l3.sweep0(prolong(w6, t3, p43)))
    lane3 = (iota((16, 128), 1) >= 48) & (iota((16, 128), 1) < 80)
    lane4 = (iota((8, 128), 1) >= 24) & (iota((8, 128), 1) < 40)
    g3m = jnp.where(lane3, g3own, 0.0)

    def own4(x):
        return jnp.where(lane4, x[24:32], 0.0)

    parts = [
        0.25 * total(y3[48:64] * g3m),
        0.25 * total(f2[48:64] * g3m),
        total(f3[48:64] * g3m),
        total(own4(l4.apply(one4))),
        total(own4(l4.apply(w6))),
        total(own4(q * w12)),
        total(own4(q * w6)),
    ]
    lane = iota((1, 128), 1)
    row = jnp.zeros((1, 128), F32)
    for n, p in enumerate(parts):
        row = jnp.where(lane == n, p, row)
    sums1 = sum_start(row, 0)

    s2w = join2(own2s[...], x2s, cps2s)
    l2 = Level(2, s2w, gx * 32 - 16, gy * 64 - 32)
    y2 = l2.sweep0(l2.sweep0(prolong(y3[40:72], t2, p32)))
    f4 = l2.sweep0(l2.sweep0(y2))
    f5 = l1.sweep0(l1.sweep0(prolong(y2[8:56], t1, p21)))
    f5 = l1.sweep0(l1.sweep0(f5))

    sums1 = sum_next(sums1, 0)

    for cp in line_g:
        cp.wait_recv()
    G3 = g_line[...]
    kg3 = l3.k * G3
    v3 = l3.sweep(kg3, kg3)
    g4 = restrict(l3.residual(v3, G3), t3, r34)
    kg4 = l4.k * g4
    e4 = kg4
    for _ in range(11):
        e4 = l4.sweep(e4, kg4)
    g2w = join2(own2g[...], x2g, cps2g)
    kg2 = l2.k * g2w
    v2 = l2.sweep(kg2, kg2)

    tot = sum_end(sums1, 0)
    a1, a2, a3, ones_total, w6_total, qw12, qw6 = (pick(tot, n) for n in range(7))
    inv = 1.0 / ones_total
    c1 = a1 * inv
    c2 = (a2 - c1 * w6_total) * inv
    c3 = 0.25 * (a3 - c1 * qw12 - c2 * qw6) * inv
    e4 = e4 + c1 * w12 + c2 * w6
    x3 = v3 + prolong(e4, t3, p43)
    for _ in range(4):
        x3 = l3.sweep(x3, kg3)
    g4 = restrict(l3.residual(x3, G3), t3, r34)
    kg4 = l4.k * g4
    e4 = kg4
    for _ in range(5):
        e4 = l4.sweep(e4, kg4)
    e4 = e4 + c3 * w6
    x3 = x3 + prolong(e4, t3, p43)
    for _ in range(2):
        x3 = l3.sweep(x3, kg3)

    lane2 = (iota((32, 128), 1) >= 32) & (iota((32, 128), 1) < 96)
    x2 = v2 + prolong(x3[40:72], t2, p32)
    r2 = l2.residual(x2, g2w)
    part = total(jnp.where(lane2, f4[16:48] * r2[16:48], 0.0)) * (1.0 / 16)
    sums2 = sum_start(jnp.zeros((1, 128), F32) + part, 1)
    for _ in range(4):
        x2 = l2.sweep(x2, kg2)
    g3 = restrict(l2.residual(x2, g2w), t2, r23)
    own3a[...] = g3
    cps3 = send3(own3a, x3a, 0)
    l3b = l3.cut(24, 88)
    l4b = l4.cut(12, 44)
    w6b = w6[12:44]

    def coarse(g3_own, buf, cps, sums, k):
        G = join3(g3_own, buf, cps)
        kgc = l3b.k * G
        v = l3b.sweep(kgc, kgc)
        gc = restrict(l3b.residual(v, G), t3, r34)
        sums = sum_next(sums, k)
        kgd = l4b.k * gc
        e = kgd
        for _ in range(5):
            e = l4b.sweep(e, kgd)
        c = sum_end(sums, k)[:, 0:1] * inv
        x = v + prolong(e + c * w6b, t3, p43)
        for _ in range(2):
            x = l3b.sweep(x, kgc)
        return x[16:48]

    e3 = coarse(g3[8:24], x3a, cps3, sums2, 1)
    x2 = x2 + prolong(e3, t2, p32)
    for _ in range(2):
        x2 = l2.sweep(x2, kg2)

    x1 = v1 + prolong(x2[8:56], t1, p21)
    r1 = l1.residual(x1, g1)
    lane1 = (iota((64, 256), 1) >= 64) & (iota((64, 256), 1) < 192)
    part = total(jnp.where(lane1, f5[16:80] * r1[16:80], 0.0)) * (1.0 / 64)
    sums3 = sum_start(jnp.zeros((1, 128), F32) + part, 2)
    for _ in range(4):
        x1 = l1.sweep(x1, kg1)
    g2 = restrict(l1.residual(x1, g1), t1, rm)
    pad = jnp.zeros((8, 128), F32)
    g2 = jnp.concatenate([pad, g2, pad], axis=0)
    kg = l2.k * g2
    g3 = restrict(l2.residual(l2.sweep(kg, kg), g2), t2, r23)
    own3b[...] = g3
    cps3 = send3(own3b, x3b, 1)
    own2h[...] = g2[16:48]
    cps2h = send2(own2h, x2h, 2)
    e3 = coarse(g3[8:24], x3b, cps3, sums3, 2)
    g2 = join2(own2h[...], x2h, cps2h)
    kg2 = l2.k * g2
    x2 = l2.sweep(kg2, kg2) + prolong(e3, t2, p32)
    for _ in range(2):
        x2 = l2.sweep(x2, kg2)
    x1 = x1 + prolong(x2[8:56], t1, p21)
    for _ in range(2):
        x1 = l1.sweep(x1, kg1)

    for t in range(2):
        y = mm(x1[:, 128 * t : 128 * t + 128], p21[...])
        for h in range(2):
            tmp0[2 * t + h, pl.ds(0, 96, 2), :] = y[:, 128 * h : 128 * h + 128]
            tmp0[2 * t + h, pl.ds(1, 96, 2), :] = y[:, 128 * h : 128 * h + 128]
    for r in range(16, 176, STEP):
        w = slice(8 + r, 8 + r + STEP)
        e = jnp.concatenate([tmp0[t, r : r + STEP, :] for t in range(4)], axis=1)
        wa[w, :] = v0[w, :] + e
    for src, dst in ((wa, wb), (wb, wa)):
        for r in range(16, 176, STEP):
            w = slice(8 + r, 8 + r + STEP)
            c, around = near4(src, r)
            dst[w, :] = 0.2 * c + kg0[w, :] + kk[w, :] * around
    for r in range(32, 160, STEP):
        w = slice(8 + r, 8 + r + STEP)
        c, around = near4(wa, r)
        sol[r - 32 : r - 32 + STEP, :] = c[:, 128:384]
        out = rhs[r - 32 : r - 32 + STEP, :] + around[:, 128:384]
        out = out - (4.0 + shf[r - 32 : r - 32 + STEP, :]) * c[:, 128:384]
        res[r - 32 : r - 32 + STEP, :] = out
    for cp in sent:
        cp.wait_send()


def tmp0_pair(ref, t, rows):
    return jnp.concatenate(
        [
            ref[2 * t + h, pl.ds(0, rows // 2, 2), :] + ref[2 * t + h, pl.ds(1, rows // 2, 2), :]
            for h in range(2)
        ],
        axis=1,
    )


def body(right_side, shift):
    v = pltpu.VMEM
    dma = pltpu.SemaphoreType.DMA
    big = v((208, 512), F32)
    scratch = (
        [big] * 7
        + [v((4, 192, 128), F32)]
        + [v((2, 128, 128), F32), v((2, 128, 128), F32), v((1, 112, 128), F32)]
        + [v((256, 128), BF16)]
        + [v((128, 128), BF16)] * 4
        + [v((128, 256), BF16), v((256, 128), BF16)]
        + [v((4, 16, 128), F32), v((112, 128), F32)] * 2
        + [v((16, 128), F32)] * 2
        + [v((2, 16, 128), F32)]
        + [v((8, 32, 128), F32)] * 3
        + [v((32, 128), F32)] * 3
        + [v((8, 24, 128), F32)] * 2
        + [v((32, 128), F32)] * 2
        + [v((3, 2, 1, 128), F32), v((3, 15, 1, 128), F32), v((3, 15, 1, 128), F32)]
        + [dma((2, 8))] * 2
        + [dma((10,))] * 4
        + [dma((3, 8))] * 2
        + [dma((2, 8))] * 2
        + [dma((3, 2, 15))] * 2
    )
    shape = jax.ShapeDtypeStruct((128, 256), F32)
    vm = pl.BlockSpec(memory_space=pltpu.VMEM)
    return pl.pallas_call(
        kernel,
        out_shape=(shape, shape),
        in_specs=[vm, vm],
        out_specs=(vm, vm),
        scratch_shapes=scratch,
        compiler_params=pltpu.CompilerParams(
            collective_id=0, has_side_effects=True, vmem_limit_bytes=32 * 1024 * 1024
        ),
        name="fcycle",
    )(right_side, shift)


def solution(mesh):
    spec = P("gx", "gy")
    return jax.shard_map(
        body, mesh=mesh, in_specs=(spec, spec), out_specs=(spec, spec), check_vma=False
    )
```

time: 803 us -> 65.3 us (0.08)
  the two profiles are of different devices: /device:TPU:104 before, /device:TPU:1 now
where the time goes in v1:
time: 65.3 us; the launch traced here: 65.2 us
  Pallas kernels  61.4 us (94%)
  local copies, waits for them, and re-layouts  3.11 us (5%)
    pallas_call x1, Pallas kernels, body(): pl.pallas_call(kernel, out_shape=(shape, shape), in_specs=[vm, vm], out_s...  61.4 us
    unnamed x6, local copies, waits for them, and re-layouts  3.11 us

profile of v1, /device:TPU:1, one launch (start us, length us, event | category | flops | bytes accessed | tf_op | source)
XLA Modules:
  0.0 65.2 jit_solution(1815590658807795523)
XLA Ops:
  0.6 0.0 copy-start
  0.6 0.9 %copy-done = f32[128,256]{1,0:T(8,128)S(1)} copy-done((f32[128,256]{1,0:T(8,128)S(1)}, f32[128,256]{1,0:T(8,128)}, u32[]{:S(2)}) %copy-start) | copy-done | bytes 131096
  1.5 0.0 copy-start.1
  1.5 0.9 %copy-done.1 = f32[128,256]{1,0:T(8,128)S(1)} copy-done((f32[128,256]{1,0:T(8,128)S(1)}, f32[128,256]{1,0:T(8,128)}, u32[]{:S(2)}) %copy-start.1) | copy-done | bytes 131096
  2.4 61.4 %fcycle.1 = (f32[128,256]{1,0:T(8,128)S(1)}, f32[128,256]{1,0:T(8,128)S(1)}) custom-call(f32[128,256]{1,0:T(8,128)S(1)} %copy-done, f32[128,256]{1,0:T(8,128)S(1)} %copy-done.1), custom_call_target="tpu_custom_call" | custom-call | tf_op jit(solution)/shard_map/fcycle/pallas_call | solution.py:622
  63.9 0.7 %copy.6 = f32[128,256]{1,0:T(8,128)} copy(f32[128,256]{1,0:T(8,128)S(1)} %get-tuple-element.4) | data formatting | bytes 262144
  64.5 0.7 %copy.7 = f32[128,256]{1,0:T(8,128)} copy(f32[128,256]{1,0:T(8,128)S(1)} %get-tuple-element.5) | data formatting | bytes 262144
Async XLA Ops:
  0.6 0.9 %copy-start = (f32[128,256]{1,0:T(8,128)S(1)}, f32[128,256]{1,0:T(8,128)}, u32[]{:S(2)}) copy-start(f32[128,256]{1,0:T(8,128)} %rhs.1) | copy-start | bytes 393220
  1.5 0.9 %copy-start.1 = (f32[128,256]{1,0:T(8,128)S(1)}, f32[128,256]{1,0:T(8,128)}, u32[]{:S(2)}) copy-start(f32[128,256]{1,0:T(8,128)} %shf.1) | copy-start | bytes 393220

commit v2 on v1

--- a/solution.py
+++ b/solution.py
@@ -97,15 +97,14 @@
 
 
 def kernel(
-    rhs, shf, sol, res,
+    rhs_in, shf_in, sol, res,
     xg, xs, kk, kg0, v0, wa, wb, tmp0,
-    t1, t2, t3,
+    t1s, t2s, t3s,
     rm, r23, r34, p43, p32, p21, r03,
     s_side, s_line, g_side, g_line, own3, own3g, ownb,
-    x2s, x2g, x2h, own2s, own2g, own2h,
-    x3a, x3b, own3a, own3b,
+    x2b, own2, x3b, own3n,
     ar_in, ar_a, ar_b,
-    e0_ss, e0_rs, s_ss, s_rs, g_ss, g_rs, x2_ss, x2_rs, x3_ss, x3_rs, ar_ss, ar_rs,
+    e0_ss, e0_rs, s_ss, s_rs, g_ss, g_rs, x2_ss, x2_rs, x3_ss, x3_rs, ar_ss, ar_rs, in_s,
 ):
     gx = lax.axis_index("gx")
     gy = lax.axis_index("gy")
@@ -131,7 +130,19 @@
     for p in partners:
         pl.semaphore_signal(barrier, inc=1, device_id=p, device_id_type=MESH)
 
+    mid = (slice(40, 168), slice(128, 384))
+    rhs, shf = xg.at[mid], xs.at[mid]
+    in_shf = pltpu.make_async_copy(shf_in, shf, in_s.at[0])
+    in_rhs = pltpu.make_async_copy(rhs_in, rhs, in_s.at[1])
+    in_shf.start()
+    in_rhs.start()
+
     sent = []
+    turn = [0]
+
+    def scratch(pool):
+        turn[0] += 1
+        return pool.at[turn[0] % pool.shape[0]]
 
     def send(src, dst, ss, rs, dev):
         cp = pltpu.make_async_remote_copy(
@@ -166,11 +177,13 @@
         for t in range(x.shape[1] // 128):
             ref[t, 0 : x.shape[0], :] = x[:, 128 * t : 128 * t + 128]
 
-    def restrict(x, ref, w):
+    def restrict(x, pool, w):
+        ref = scratch(pool)
         put(ref, x)
         return mm(pair_rows(ref, x.shape[0], x.shape[1]), w[...])
 
-    def prolong(e, ref, w):
+    def prolong(e, pool, w):
+        ref = scratch(pool)
         y = mm(e, w[...])
         m = y.shape[0]
         out = []
@@ -181,24 +194,30 @@
             out.append(ref[t, 0 : 2 * m, :])
         return jnp.concatenate(out, axis=1) if len(out) > 1 else out[0]
 
+    zero8 = jnp.zeros((8, 512), F32)
+    for ref in (kg0, v0, wa, wb):
+        ref[0:8, :] = zero8
+        ref[200:208, :] = zero8
+    for ref in (xs, xg):
+        ref[8:16, :] = zero8
+        ref[192:200, :] = zero8
+
+    in_shf.wait()
     s0 = shf[...]
-    for t in range(2):
-        tmp0[t, 0:128, :] = s0[:, 128 * t : 128 * t + 128]
+    put(tmp0, s0)
     acc = pair_rows(tmp0, 128, 256)
-    put(t1, acc)
-    acc = pair_rows(t1, 64, 256)
-    put(t2, acc)
-    acc = pair_rows(t2, 32, 256)
-    own3[...] = mm(acc, r03[...])
-    put(t1, s0)
-    s1own = mm(pair_rows(t1, 128, 256), rm[...])
-    put(t2, s1own)
-    s2own = mm(pair_rows(t2, 64, 128), r34[...])
-    own2s[...] = pltpu.roll(s2own, 32, axis=1)
+    s1own = mm(acc, rm[...])
+    ref1, ref2 = scratch(t1s), scratch(t2s)
+    put(ref1, acc)
+    acc = pair_rows(ref1, 64, 256)
+    put(ref2, acc)
+    own3[...] = mm(pair_rows(ref2, 32, 256), r03[...])
+    own2[0] = pltpu.roll(restrict(s1own, t1s, r34), 32, axis=1)
+    in_rhs.wait()
 
     pl.semaphore_wait(barrier, len(partners))
 
-    ROWS = {-1: (0, 32, 160, 192), 1: (96, 128, 0, 32), 0: (0, 128, 32, 160)}
+    ROWS = {-1: (0, 24, 160, 184), 1: (104, 128, 8, 32), 0: (0, 128, 32, 160)}
     COLS = {-1: (0, 128, 384, 512), 1: (128, 256, 0, 128), 0: (0, 256, 128, 384)}
     first = []
 
@@ -241,7 +260,9 @@
 
     SRC2 = {-1: (0, 16), 1: (16, 32), 0: (0, 32)}
 
-    def send2(src, buf, k):
+    def send2(x, k):
+        own2[k] = x
+        src, buf = own2.at[k], x2b.at[k]
         cps = []
         for n, (dz, dy) in enumerate(AROUND):
             a, b = SRC2[dz]
@@ -258,9 +279,10 @@
         out = jnp.where(lane < lo, pltpu.roll(left, 128 - move, axis=1), mid)
         return jnp.where(lane >= hi, pltpu.roll(right, move, axis=1), out)
 
-    def join2(own, buf, cps):
+    def join2(k, cps):
         for cp in cps:
             cp.wait_recv()
+        own, buf = own2[k], x2b.at[k]
         dn, up, rt, lf, dr, dl, ur, ul = range(8)
         return jnp.concatenate(
             [
@@ -273,7 +295,9 @@
 
     SRC3 = {-1: (8, 32), 1: (0, 24), 0: (8, 24)}
 
-    def send3(src, buf, k):
+    def send3(x, k):
+        own3n[k] = x
+        src, buf = own3n.at[k], x3b.at[k]
         cps = []
         for n, (dz, dy) in enumerate(AROUND):
             a, b = SRC3[dz]
@@ -285,9 +309,10 @@
             )
         return cps
 
-    def join3(own, buf, cps):
+    def join3(k, cps):
         for cp in cps:
             cp.wait_recv()
+        own, buf = own3n[k, 8:24], x3b.at[k]
         dn, up, rt, lf, dr, dl, ur, ul = range(8)
         return jnp.concatenate(
             [
@@ -329,13 +354,11 @@
     side_s = side_send(own3, s_side, s_ss, s_rs)
     border(1)
     border(0)
-    cps2s = send2(own2s, x2s, 0)
-    xs[8 + 32 : 8 + 160, 128:384] = s0
-    xg[8 + 32 : 8 + 160, 128:384] = rhs[...]
-    zero8 = jnp.zeros((8, 512), F32)
-    for ref in (kg0, v0, wa, wb):
-        ref[0:8, :] = zero8
-        ref[200:208, :] = zero8
+    cps2s = send2(own2[0], 0)
+    s_row = side_join(own3[...], s_side, side_s)
+    ownb[0] = s_row
+    line_s = line_send(ownb.at[0], s_line, s_ss, s_rs)
+    s_line[48:64] = s_row
 
     row0 = gx * 128 - 32
     col0 = gy * 256 - 128
@@ -366,12 +389,8 @@
         axis=1,
     )
     l1 = Level(1, s1, gx * 64 - 16, gy * 128 - 64)
-    s2 = restrict(s1, t1, rm)
-
-    s_row = side_join(own3[...], s_side, side_s)
-    ownb[0] = s_row
-    line_s = line_send(ownb.at[0], s_line, s_ss, s_rs)
-    s_line[48:64] = s_row
+    s2 = restrict(s1, t1s, rm)
+    l2a = Level(2, s2, gx * 32 - 8, gy * 64 - 32)
 
     for cp in first[8:]:
         cp.wait_recv()
@@ -392,27 +411,20 @@
 
     kg1 = l1.k * g1
     v1 = l1.sweep(kg1, kg1)
-    g2 = restrict(l1.residual(v1, g1), t1, rm)
-    l2a = Level(2, s2, gx * 32 - 8, gy * 64 - 32)
+    g2 = restrict(l1.residual(v1, g1), t1s, rm)
     kg = l2a.k * g2
     r2 = l2a.residual(l2a.sweep(kg, kg), g2)
-    own2g[...] = g2[8:40]
-    g3 = restrict(r2, t2, r23)
+    g3 = restrict(r2, t2s, r23)
     g3own = g3[4:20]
     own3g[...] = g3own
     side_g = side_send(own3g, g_side, g_ss, g_rs)
-    cps2g = send2(own2g, x2g, 1)
+    cps2g = send2(g2[8:40], 1)
 
     for cp in line_s:
         cp.wait_recv()
     l3 = Level(3, s_line[...], gx * 16 - 48, gy * 32 - 48)
-    s4 = restrict(s_line[...], t3, r34)
+    s4 = restrict(s_line[...], t3s, r34)
     l4 = Level(4, s4, gx * 8 - 24, gy * 16 - 24, iota((56, 128), 1) < 64)
-
-    g_row = side_join(g3own, g_side, side_g)
-    ownb[1] = g_row
-    line_g = line_send(ownb.at[1], g_line, g_ss, g_rs)
-    g_line[48:64] = g_row
 
     one4 = jnp.where(l4.ok, 1.0, 0.0)
     one3 = jnp.where(l3.ok, 1.0, 0.0)
@@ -424,13 +436,13 @@
         w12 = l4.sweep0(w12)
     y3 = l3.sweep0(l3.sweep0(one3))
     u = l3.sweep0(l3.sweep0(y3))
-    q = 4.0 * restrict(jnp.where(l3.ok, l3.apply(u), 0.0), t3, r34)
+    q = 4.0 * restrict(jnp.where(l3.ok, l3.apply(u), 0.0), t3s, r34)
     kq = l4.k * q
     z = kq
     for _ in range(11):
         z = l4.sweep(z, kq)
-    f3 = l3.sweep0(l3.sweep0(u - 0.25 * prolong(z, t3, p43)))
-    f2 = l3.sweep0(l3.sweep0(prolong(w6, t3, p43)))
+    f3 = l3.sweep0(l3.sweep0(u - 0.25 * prolong(z, t3s, p43)))
+    f2 = l3.sweep0(l3.sweep0(prolong(w6, t3s, p43)))
     lane3 = (iota((16, 128), 1) >= 48) & (iota((16, 128), 1) < 80)
     lane4 = (iota((8, 128), 1) >= 24) & (iota((8, 128), 1) < 40)
     g3m = jnp.where(lane3, g3own, 0.0)
@@ -453,12 +465,34 @@
         row = jnp.where(lane == n, p, row)
     sums1 = sum_start(row, 0)
 
-    s2w = join2(own2s[...], x2s, cps2s)
+    g_row = side_join(g3own, g_side, side_g)
+    ownb[1] = g_row
+    line_g = line_send(ownb.at[1], g_line, g_ss, g_rs)
+    g_line[48:64] = g_row
+
+    def down2(x):
+        pad = jnp.zeros((8, 128), F32)
+        g = jnp.concatenate([pad, x, pad], axis=0)
+        kg = l2.k * g
+        g3 = restrict(l2.residual(l2.sweep(kg, kg), g), t2s, r23)
+        return g, g3
+
+    s2w = join2(0, cps2s)
     l2 = Level(2, s2w, gx * 32 - 16, gy * 64 - 32)
-    y2 = l2.sweep0(l2.sweep0(prolong(y3[40:72], t2, p32)))
+    lane1 = (iota((64, 256), 1) >= 64) & (iota((64, 256), 1) < 192)
+    lane2 = (iota((32, 128), 1) >= 32) & (iota((32, 128), 1) < 96)
+    y2 = l2.sweep0(l2.sweep0(prolong(y3[40:72], t2s, p32)))
+    z2 = l2.sweep0(l2.sweep0(prolong(f2[40:72], t2s, p32)))
     f4 = l2.sweep0(l2.sweep0(y2))
-    f5 = l1.sweep0(l1.sweep0(prolong(y2[8:56], t1, p21)))
+    f5 = l1.sweep0(l1.sweep0(prolong(y2[8:56], t1s, p21)))
     f5 = l1.sweep0(l1.sweep0(f5))
+    z1 = prolong(z2[8:56], t1s, p21)
+    p5r = total(jnp.where(lane1, f5[16:80] * l1.apply(z1)[16:80], 0.0)) * (-1.0 / 64)
+    w1 = l1.sweep0(l1.sweep0(z1))
+    d1 = l1.sweep0(l1.sweep0(w1))
+    h2, h3 = down2(restrict(-l1.apply(d1), t1s, rm))
+    cps3r = send3(h3, 2)
+    cps2r = send2(h2[16:48], 3)
 
     sums1 = sum_next(sums1, 0)
 
@@ -467,12 +501,12 @@
     G3 = g_line[...]
     kg3 = l3.k * G3
     v3 = l3.sweep(kg3, kg3)
-    g4 = restrict(l3.residual(v3, G3), t3, r34)
+    g4 = restrict(l3.residual(v3, G3), t3s, r34)
     kg4 = l4.k * g4
     e4 = kg4
     for _ in range(11):
         e4 = l4.sweep(e4, kg4)
-    g2w = join2(own2g[...], x2g, cps2g)
+    g2w = join2(1, cps2g)
     kg2 = l2.k * g2w
     v2 = l2.sweep(kg2, kg2)
 
@@ -483,79 +517,79 @@
     c2 = (a2 - c1 * w6_total) * inv
     c3 = 0.25 * (a3 - c1 * qw12 - c2 * qw6) * inv
     e4 = e4 + c1 * w12 + c2 * w6
-    x3 = v3 + prolong(e4, t3, p43)
+    x3 = v3 + prolong(e4, t3s, p43)
     for _ in range(4):
         x3 = l3.sweep(x3, kg3)
-    g4 = restrict(l3.residual(x3, G3), t3, r34)
+    g4 = restrict(l3.residual(x3, G3), t3s, r34)
     kg4 = l4.k * g4
     e4 = kg4
     for _ in range(5):
         e4 = l4.sweep(e4, kg4)
     e4 = e4 + c3 * w6
-    x3 = x3 + prolong(e4, t3, p43)
+    x3 = x3 + prolong(e4, t3s, p43)
     for _ in range(2):
         x3 = l3.sweep(x3, kg3)
 
-    lane2 = (iota((32, 128), 1) >= 32) & (iota((32, 128), 1) < 96)
-    x2 = v2 + prolong(x3[40:72], t2, p32)
+    x2 = v2 + prolong(x3[40:72], t2s, p32)
     r2 = l2.residual(x2, g2w)
-    part = total(jnp.where(lane2, f4[16:48] * r2[16:48], 0.0)) * (1.0 / 16)
-    sums2 = sum_start(jnp.zeros((1, 128), F32) + part, 1)
+    p4 = total(jnp.where(lane2, f4[16:48] * r2[16:48], 0.0)) * (1.0 / 16)
+    sums2 = sum_start(jnp.where(lane == 0, p4, jnp.where(lane == 1, p5r, 0.0)), 1)
     for _ in range(4):
         x2 = l2.sweep(x2, kg2)
-    g3 = restrict(l2.residual(x2, g2w), t2, r23)
-    own3a[...] = g3
-    cps3 = send3(own3a, x3a, 0)
+    cps3 = send3(restrict(l2.residual(x2, g2w), t2s, r23), 0)
     l3b = l3.cut(24, 88)
     l4b = l4.cut(12, 44)
-    w6b = w6[12:44]
-
-    def coarse(g3_own, buf, cps, sums, k):
-        G = join3(g3_own, buf, cps)
+
+    def coarse(G):
         kgc = l3b.k * G
         v = l3b.sweep(kgc, kgc)
-        gc = restrict(l3b.residual(v, G), t3, r34)
-        sums = sum_next(sums, k)
-        kgd = l4b.k * gc
+        kgd = l4b.k * restrict(l3b.residual(v, G), t3s, r34)
         e = kgd
         for _ in range(5):
             e = l4b.sweep(e, kgd)
-        c = sum_end(sums, k)[:, 0:1] * inv
-        x = v + prolong(e + c * w6b, t3, p43)
+        x = v + prolong(e, t3s, p43)
         for _ in range(2):
             x = l3b.sweep(x, kgc)
         return x[16:48]
 
-    e3 = coarse(g3[8:24], x3a, cps3, sums2, 1)
-    x2 = x2 + prolong(e3, t2, p32)
+    def up2(e3, g):
+        kg = l2.k * g
+        x = l2.sweep(kg, kg) + prolong(e3, t2s, p32)
+        for _ in range(2):
+            x = l2.sweep(x, kg)
+        return x
+
+    e3 = coarse(join3(2, cps3r))
+    x2r = up2(e3, join2(3, cps2r))
+    x1r = l1.sweep0(l1.sweep0(d1 + prolong(x2r[8:56], t1s, p21)))
+
+    x2 = x2 + prolong(coarse(join3(0, cps3)), t2s, p32)
     for _ in range(2):
         x2 = l2.sweep(x2, kg2)
 
-    x1 = v1 + prolong(x2[8:56], t1, p21)
+    x1 = v1 + prolong(x2[8:56], t1s, p21)
     r1 = l1.residual(x1, g1)
-    lane1 = (iota((64, 256), 1) >= 64) & (iota((64, 256), 1) < 192)
-    part = total(jnp.where(lane1, f5[16:80] * r1[16:80], 0.0)) * (1.0 / 64)
-    sums3 = sum_start(jnp.zeros((1, 128), F32) + part, 2)
+    p5 = total(jnp.where(lane1, f5[16:80] * r1[16:80], 0.0)) * (1.0 / 64)
+    sums3 = sum_start(jnp.zeros((1, 128), F32) + p5, 2)
     for _ in range(4):
         x1 = l1.sweep(x1, kg1)
-    g2 = restrict(l1.residual(x1, g1), t1, rm)
-    pad = jnp.zeros((8, 128), F32)
-    g2 = jnp.concatenate([pad, g2, pad], axis=0)
-    kg = l2.k * g2
-    g3 = restrict(l2.residual(l2.sweep(kg, kg), g2), t2, r23)
-    own3b[...] = g3
-    cps3 = send3(own3b, x3b, 1)
-    own2h[...] = g2[16:48]
-    cps2h = send2(own2h, x2h, 2)
-    e3 = coarse(g3[8:24], x3b, cps3, sums3, 2)
-    g2 = join2(own2h[...], x2h, cps2h)
-    kg2 = l2.k * g2
-    x2 = l2.sweep(kg2, kg2) + prolong(e3, t2, p32)
-    for _ in range(2):
-        x2 = l2.sweep(x2, kg2)
-    x1 = x1 + prolong(x2[8:56], t1, p21)
+    g2, g3 = down2(restrict(l1.residual(x1, g1), t1s, rm))
+    cps3 = send3(g3, 1)
+    cps2h = send2(g2[16:48], 2)
+    sums2 = sum_next(sums2, 1)
+    sums3 = sum_next(sums3, 2)
+    e3 = coarse(join3(1, cps3))
+    x2 = up2(e3, join2(2, cps2h))
+    x1 = x1 + prolong(x2[8:56], t1s, p21)
     for _ in range(2):
         x1 = l1.sweep(x1, kg1)
+    tot2 = sum_end(sums2, 1)
+    c4 = pick(tot2, 0) * inv
+    p5r = pick(tot2, 1)
+    x1 = x1 + c4 * x1r
+    tot3 = sum_end(sums3, 2)
+    c5 = (tot3[:, 0:1] + c4 * p5r) * inv
+    x1 = x1 + c5 * w1
 
     for t in range(2):
         y = mm(x1[:, 128 * t : 128 * t + 128], p21[...])
@@ -599,34 +633,33 @@
     scratch = (
         [big] * 7
         + [v((4, 192, 128), F32)]
-        + [v((2, 128, 128), F32), v((2, 128, 128), F32), v((1, 112, 128), F32)]
+        + [v((4, 2, 128, 128), F32), v((4, 2, 128, 128), F32), v((4, 1, 112, 128), F32)]
         + [v((256, 128), BF16)]
         + [v((128, 128), BF16)] * 4
         + [v((128, 256), BF16), v((256, 128), BF16)]
         + [v((4, 16, 128), F32), v((112, 128), F32)] * 2
         + [v((16, 128), F32)] * 2
         + [v((2, 16, 128), F32)]
-        + [v((8, 32, 128), F32)] * 3
-        + [v((32, 128), F32)] * 3
-        + [v((8, 24, 128), F32)] * 2
-        + [v((32, 128), F32)] * 2
+        + [v((4, 8, 32, 128), F32), v((4, 32, 128), F32)]
+        + [v((3, 8, 24, 128), F32), v((3, 32, 128), F32)]
         + [v((3, 2, 1, 128), F32), v((3, 15, 1, 128), F32), v((3, 15, 1, 128), F32)]
         + [dma((2, 8))] * 2
         + [dma((10,))] * 4
+        + [dma((4, 8))] * 2
         + [dma((3, 8))] * 2
-        + [dma((2, 8))] * 2
         + [dma((3, 2, 15))] * 2
+        + [dma((2,))]
     )
     shape = jax.ShapeDtypeStruct((128, 256), F32)
     vm = pl.BlockSpec(memory_space=pltpu.VMEM)
     return pl.pallas_call(
         kernel,
         out_shape=(shape, shape),
-        in_specs=[vm, vm],
+        in_specs=[pl.BlockSpec(memory_space=pl.ANY)] * 2,
         out_specs=(vm, vm),
         scratch_shapes=scratch,
         compiler_params=pltpu.CompilerParams(
-            collective_id=0, has_side_effects=True, vmem_limit_bytes=32 * 1024 * 1024
+            collective_id=0, has_side_effects=True, vmem_limit_bytes=40 * 1024 * 1024
         ),
         name="fcycle",
     )(right_side, shift)

time: 65.3 us -> 55 us (0.84)
  Pallas kernels: 61.4 us -> 51.1 us
    pallas_call x1, Pallas kernels: 61.4 us -> 51.1 us  [body(): pl.pallas_call(kernel, out_shape=(shape, shape), in_specs=[pl.BlockSpec(m...]
where the time goes in v2:
time: 55 us; the launch traced here: 54.9 us
  Pallas kernels  51.1 us (93%)
  local copies, waits for them, and re-layouts  3.11 us (6%)
  between operations  0.65 us (1%)
    pallas_call x1, Pallas kernels, body(): pl.pallas_call(kernel, out_shape=(shape, shape), in_specs=[pl.BlockSpec(m...  51.1 us
    unnamed x6, local copies, waits for them, and re-layouts  3.11 us

profile of v2, /device:TPU:1, one launch (start us, length us, event | category | flops | bytes accessed | tf_op | source)
XLA Modules:
  0.0 54.9 jit_solution(5131473715263738591)
XLA Ops:
  0.6 0.0 copy-start
  0.6 0.9 %copy-done = f32[128,256]{1,0:T(8,128)S(1)} copy-done((f32[128,256]{1,0:T(8,128)S(1)}, f32[128,256]{1,0:T(8,128)}, u32[]{:S(2)}) %copy-start) | copy-done | bytes 131096
  1.5 0.0 copy-start.1
  1.5 0.9 %copy-done.1 = f32[128,256]{1,0:T(8,128)S(1)} copy-done((f32[128,256]{1,0:T(8,128)S(1)}, f32[128,256]{1,0:T(8,128)}, u32[]{:S(2)}) %copy-start.1) | copy-done | bytes 131096
  2.4 51.1 %fcycle.1 = (f32[128,256]{1,0:T(8,128)S(1)}, f32[128,256]{1,0:T(8,128)S(1)}) custom-call(f32[128,256]{1,0:T(8,128)S(1)} %copy-done, f32[128,256]{1,0:T(8,128)S(1)} %copy-done.1), custom_call_target="tpu_custom_call" | custom-call | tf_op jit(solution)/shard_map/fcycle/pallas_call | solution.py:655
  53.6 0.7 %copy.6 = f32[128,256]{1,0:T(8,128)} copy(f32[128,256]{1,0:T(8,128)S(1)} %get-tuple-element.4) | data formatting | bytes 262144
  54.2 0.7 %copy.7 = f32[128,256]{1,0:T(8,128)} copy(f32[128,256]{1,0:T(8,128)S(1)} %get-tuple-element.5) | data formatting | bytes 262144
Async XLA Ops:
  0.6 0.9 %copy-start = (f32[128,256]{1,0:T(8,128)S(1)}, f32[128,256]{1,0:T(8,128)}, u32[]{:S(2)}) copy-start(f32[128,256]{1,0:T(8,128)} %rhs_in.1) | copy-start | bytes 393220
  1.5 0.9 %copy-start.1 = (f32[128,256]{1,0:T(8,128)S(1)}, f32[128,256]{1,0:T(8,128)}, u32[]{:S(2)}) copy-start(f32[128,256]{1,0:T(8,128)} %shf_in.1) | copy-start | bytes 393220

commit v3 on v2

--- a/solution.py
+++ b/solution.py
@@ -102,7 +102,7 @@
     t1s, t2s, t3s,
     rm, r23, r34, p43, p32, p21, r03,
     s_side, s_line, g_side, g_line, own3, own3g, ownb,
-    x2b, own2, x3b, own3n,
+    x2b, own2, x3b, own3n, own3p,
     ar_in, ar_a, ar_b,
     e0_ss, e0_rs, s_ss, s_rs, g_ss, g_rs, x2_ss, x2_rs, x3_ss, x3_rs, ar_ss, ar_rs, in_s,
 ):
@@ -293,35 +293,43 @@
             axis=0,
         )
 
-    SRC3 = {-1: (8, 32), 1: (0, 24), 0: (8, 24)}
+    def pack3(x, lo):
+        lane = iota((8, 128), 1)
+        a, b, c = (x[lo + 8 * n : lo + 8 * n + 8] for n in range(3))
+        out = jnp.where(lane < 64, pltpu.roll(b, 112, axis=1), pltpu.roll(c, 16, axis=1))
+        return jnp.where(lane < 32, pltpu.roll(a, 80, axis=1), out)
 
     def send3(x, k):
         own3n[k] = x
-        src, buf = own3n.at[k], x3b.at[k]
-        cps = []
-        for n, (dz, dy) in enumerate(AROUND):
-            a, b = SRC3[dz]
-            cps.append(
-                send(
-                    src.at[a:b], buf.at[n, 0 : b - a],
-                    x3_ss.at[k, n], x3_rs.at[k, n], near(dz, dy),
-                )
+        own3p[k, 0] = pack3(x, 8)
+        own3p[k, 1] = pack3(x, 0)
+        return [
+            send(
+                own3p.at[k, 1 if dz == 1 else 0], x3b.at[k, n],
+                x3_ss.at[k, n], x3_rs.at[k, n], near(dz, dy),
             )
-        return cps
-
-    def join3(k, cps):
+            for n, (dz, dy) in enumerate(AROUND)
+        ]
+
+    def take3(k, cps):
         for cp in cps:
             cp.wait_recv()
-        own, buf = own3n[k, 8:24], x3b.at[k]
-        dn, up, rt, lf, dr, dl, ur, ul = range(8)
-        return jnp.concatenate(
-            [
-                lanes3(buf[ul], buf[up], buf[ur], 48, 80, 32),
-                lanes3(buf[lf, 0:16], own, buf[rt, 0:16], 48, 80, 32),
-                lanes3(buf[dl], buf[dn], buf[dr], 48, 80, 32),
-            ],
-            axis=0,
-        )
+        return [own3n[k, 8:24]] + [x3b[k, n] for n in range(8)]
+
+    def join3(own, dn, up, rt, lf, dr, dl, ur, ul):
+        lane = iota((8, 128), 1)
+
+        def at(x, n, dest):
+            move = (dest - 32 * n) % 128
+            return pltpu.roll(x, move, axis=1) if move else x
+
+        rows = []
+        for left, centre, right, count in ((ul, up, ur, 3), (lf, None, rt, 2), (dl, dn, dr, 3)):
+            for n in range(count):
+                c = own[8 * n : 8 * n + 8] if centre is None else at(centre, n, 48)
+                out = jnp.where(lane < 80, c, at(right, n, 80))
+                rows.append(jnp.where(lane < 48, at(left, n, 16), out))
+        return jnp.concatenate(rows, axis=0)
 
     def sum_start(row, k):
         ar_in[k, 0] = row
@@ -470,76 +478,6 @@
     line_g = line_send(ownb.at[1], g_line, g_ss, g_rs)
     g_line[48:64] = g_row
 
-    def down2(x):
-        pad = jnp.zeros((8, 128), F32)
-        g = jnp.concatenate([pad, x, pad], axis=0)
-        kg = l2.k * g
-        g3 = restrict(l2.residual(l2.sweep(kg, kg), g), t2s, r23)
-        return g, g3
-
-    s2w = join2(0, cps2s)
-    l2 = Level(2, s2w, gx * 32 - 16, gy * 64 - 32)
-    lane1 = (iota((64, 256), 1) >= 64) & (iota((64, 256), 1) < 192)
-    lane2 = (iota((32, 128), 1) >= 32) & (iota((32, 128), 1) < 96)
-    y2 = l2.sweep0(l2.sweep0(prolong(y3[40:72], t2s, p32)))
-    z2 = l2.sweep0(l2.sweep0(prolong(f2[40:72], t2s, p32)))
-    f4 = l2.sweep0(l2.sweep0(y2))
-    f5 = l1.sweep0(l1.sweep0(prolong(y2[8:56], t1s, p21)))
-    f5 = l1.sweep0(l1.sweep0(f5))
-    z1 = prolong(z2[8:56], t1s, p21)
-    p5r = total(jnp.where(lane1, f5[16:80] * l1.apply(z1)[16:80], 0.0)) * (-1.0 / 64)
-    w1 = l1.sweep0(l1.sweep0(z1))
-    d1 = l1.sweep0(l1.sweep0(w1))
-    h2, h3 = down2(restrict(-l1.apply(d1), t1s, rm))
-    cps3r = send3(h3, 2)
-    cps2r = send2(h2[16:48], 3)
-
-    sums1 = sum_next(sums1, 0)
-
-    for cp in line_g:
-        cp.wait_recv()
-    G3 = g_line[...]
-    kg3 = l3.k * G3
-    v3 = l3.sweep(kg3, kg3)
-    g4 = restrict(l3.residual(v3, G3), t3s, r34)
-    kg4 = l4.k * g4
-    e4 = kg4
-    for _ in range(11):
-        e4 = l4.sweep(e4, kg4)
-    g2w = join2(1, cps2g)
-    kg2 = l2.k * g2w
-    v2 = l2.sweep(kg2, kg2)
-
-    tot = sum_end(sums1, 0)
-    a1, a2, a3, ones_total, w6_total, qw12, qw6 = (pick(tot, n) for n in range(7))
-    inv = 1.0 / ones_total
-    c1 = a1 * inv
-    c2 = (a2 - c1 * w6_total) * inv
-    c3 = 0.25 * (a3 - c1 * qw12 - c2 * qw6) * inv
-    e4 = e4 + c1 * w12 + c2 * w6
-    x3 = v3 + prolong(e4, t3s, p43)
-    for _ in range(4):
-        x3 = l3.sweep(x3, kg3)
-    g4 = restrict(l3.residual(x3, G3), t3s, r34)
-    kg4 = l4.k * g4
-    e4 = kg4
-    for _ in range(5):
-        e4 = l4.sweep(e4, kg4)
-    e4 = e4 + c3 * w6
-    x3 = x3 + prolong(e4, t3s, p43)
-    for _ in range(2):
-        x3 = l3.sweep(x3, kg3)
-
-    x2 = v2 + prolong(x3[40:72], t2s, p32)
-    r2 = l2.residual(x2, g2w)
-    p4 = total(jnp.where(lane2, f4[16:48] * r2[16:48], 0.0)) * (1.0 / 16)
-    sums2 = sum_start(jnp.where(lane == 0, p4, jnp.where(lane == 1, p5r, 0.0)), 1)
-    for _ in range(4):
-        x2 = l2.sweep(x2, kg2)
-    cps3 = send3(restrict(l2.residual(x2, g2w), t2s, r23), 0)
-    l3b = l3.cut(24, 88)
-    l4b = l4.cut(12, 44)
-
     def coarse(G):
         kgc = l3b.k * G
         v = l3b.sweep(kgc, kgc)
@@ -552,6 +490,14 @@
             x = l3b.sweep(x, kgc)
         return x[16:48]
 
+    def down2(x):
+        pad = jnp.zeros((8, 128), F32)
+        g = jnp.concatenate([pad, x, pad], axis=0)
+        kg = l2.k * g
+        v = l2.sweep(kg, kg)
+        r = l2.residual(v, g)
+        return g, v, r, restrict(r, t2s, r23)
+
     def up2(e3, g):
         kg = l2.k * g
         x = l2.sweep(kg, kg) + prolong(e3, t2s, p32)
@@ -559,37 +505,138 @@
             x = l2.sweep(x, kg)
         return x
 
-    e3 = coarse(join3(2, cps3r))
-    x2r = up2(e3, join2(3, cps2r))
-    x1r = l1.sweep0(l1.sweep0(d1 + prolong(x2r[8:56], t1s, p21)))
-
-    x2 = x2 + prolong(coarse(join3(0, cps3)), t2s, p32)
+    l3b = l3.cut(24, 88)
+    l4b = l4.cut(12, 44)
+    lane1 = (iota((64, 256), 1) >= 64) & (iota((64, 256), 1) < 192)
+    lane2 = (iota((32, 128), 1) >= 32) & (iota((32, 128), 1) < 96)
+
+    def dot1(a, b):
+        return total(jnp.where(lane1, a[16:80] * b[16:80], 0.0))
+
+    def dot2(a, b):
+        return total(jnp.where(lane2, a[16:48] * b[16:48], 0.0))
+
+    def dot3(a, b):
+        return total(jnp.where(lane3, a * b, 0.0))
+
+    ra, rb = prolong(w12, t3s, p43), prolong(w6, t3s, p43)
+    for _ in range(4):
+        ra, rb = l3.sweep0(ra), l3.sweep0(rb)
+    ka = l4.k * restrict(-l3.apply(ra), t3s, r34)
+    kb = l4.k * restrict(-l3.apply(rb), t3s, r34)
+    ea, eb = ka, kb
+    for _ in range(5):
+        ea, eb = l4.sweep(ea, ka), l4.sweep(eb, kb)
+    ra, rb = ra + prolong(ea, t3s, p43), rb + prolong(eb, t3s, p43)
+    for _ in range(2):
+        ra, rb = l3.sweep0(ra), l3.sweep0(rb)
+
+    s2w = join2(0, cps2s)
+    l2 = Level(2, s2w, gx * 32 - 16, gy * 64 - 32)
+    start2 = [prolong(r[40:72], t2s, p32) for r in (ra, rb, f2)]
+    after2 = start2
+    for _ in range(4):
+        after2 = [l2.sweep0(x) for x in after2]
+    h_of = [restrict(-l2.apply(x), t2s, r23) for x in after2]
+    cps_of = [send3(h, 3 + n) for n, h in enumerate(h_of)]
+    y2 = l2.sweep0(l2.sweep0(prolong(y3[40:72], t2s, p32)))
+    f5 = l1.sweep0(l1.sweep0(prolong(y2[8:56], t1s, p21)))
+    f5 = l1.sweep0(l1.sweep0(f5)) * (1.0 / 64)
+    ga, va, ta, ha = down2(4.0 * restrict(l1.apply(f5), t1s, rm))
+    ha = 4.0 * ha
+    cpsa = send3(ha, 6)
+    f4 = l2.sweep0(l2.sweep0(y2)) * (1.0 / 16)
+    p4_of = [-dot2(f4, l2.apply(x)) for x in start2]
+    p54 = -dot3(ha[8:24], f2[48:64])
+
+    sums1 = sum_next(sums1, 0)
+
+    g2w = join2(1, cps2g)
+    kg2 = l2.k * g2w
+    v2 = l2.sweep(kg2, kg2)
+    pv = dot1(f5, l1.residual(v1, g1)) - dot2(va, g2w)
+    for cp in line_g:
+        cp.wait_recv()
+    G3 = g_line[...]
+    kg3 = l3.k * G3
+    v3 = l3.sweep(kg3, kg3)
+    kg4 = l4.k * restrict(l3.residual(v3, G3), t3s, r34)
+    e4 = kg4
+    for _ in range(11):
+        e4 = l4.sweep(e4, kg4)
+    x3 = v3 + prolong(e4, t3s, p43)
+    for _ in range(4):
+        x3 = l3.sweep(x3, kg3)
+    kg4 = l4.k * restrict(l3.residual(x3, G3), t3s, r34)
+    e4 = kg4
+    for _ in range(5):
+        e4 = l4.sweep(e4, kg4)
+    x3 = x3 + prolong(e4, t3s, p43)
+    for _ in range(2):
+        x3 = l3.sweep(x3, kg3)
+
+    x2 = v2 + prolong(x3[40:72], t2s, p32)
+    p4 = dot2(f4, l2.residual(x2, g2w))
+    for _ in range(4):
+        x2 = l2.sweep(x2, kg2)
+    g3 = restrict(l2.residual(x2, g2w), t2s, r23)
+    cps3 = send3(g3, 0)
+    ma = coarse(join3(*take3(6, cpsa)))[8:24]
+    p5 = pv - dot2(ta, x2) - dot3(ma, g3[8:24])
+    p5_of = [
+        -dot2(ta, x) - dot3(ma, h[8:24]) for x, h in zip(after2, h_of)
+    ]
+    row = jnp.zeros((1, 128), F32)
+    for n, p in enumerate([p4, *p4_of, p5, *p5_of, p54]):
+        row = jnp.where(lane == n, p, row)
+    sums2 = sum_start(row, 1)
+
+    z2 = l2.sweep0(l2.sweep0(prolong(f2[40:72], t2s, p32)))
+    z1 = prolong(z2[8:56], t1s, p21)
+    w1 = l1.sweep0(l1.sweep0(z1))
+    d1 = l1.sweep0(l1.sweep0(w1))
+    h2, _, _, h3 = down2(restrict(-l1.apply(d1), t1s, rm))
+    cps3r = send3(h3, 2)
+    cps2r = send2(h2[16:48], 3)
+
+    tot = sum_end(sums1, 0)
+    a1, a2, a3, ones_total, w6_total, qw12, qw6 = (pick(tot, n) for n in range(7))
+    inv = 1.0 / ones_total
+    c1 = a1 * inv
+    c2 = (a2 - c1 * w6_total) * inv
+    c3 = 0.25 * (a3 - c1 * qw12 - c2 * qw6) * inv
+
+    def with_constants(x, parts):
+        return ((x + c1 * parts[0]) + c2 * parts[1]) + c3 * parts[2]
+
+    x2 = with_constants(x2, after2)
+    parts = [take3(3 + n, cps) for n, cps in enumerate(cps_of)]
+    G = [with_constants(b, p) for b, p in zip(take3(0, cps3), zip(*parts))]
+    x2 = x2 + prolong(coarse(join3(*G)), t2s, p32)
     for _ in range(2):
         x2 = l2.sweep(x2, kg2)
 
     x1 = v1 + prolong(x2[8:56], t1s, p21)
-    r1 = l1.residual(x1, g1)
-    p5 = total(jnp.where(lane1, f5[16:80] * r1[16:80], 0.0)) * (1.0 / 64)
-    sums3 = sum_start(jnp.zeros((1, 128), F32) + p5, 2)
     for _ in range(4):
         x1 = l1.sweep(x1, kg1)
-    g2, g3 = down2(restrict(l1.residual(x1, g1), t1s, rm))
+    g2, _, _, g3 = down2(restrict(l1.residual(x1, g1), t1s, rm))
     cps3 = send3(g3, 1)
     cps2h = send2(g2[16:48], 2)
     sums2 = sum_next(sums2, 1)
-    sums3 = sum_next(sums3, 2)
-    e3 = coarse(join3(1, cps3))
+    e3 = coarse(join3(*take3(2, cps3r)))
+    x2r = up2(e3, join2(3, cps2r))
+    x1r = l1.sweep0(l1.sweep0(d1 + prolong(x2r[8:56], t1s, p21)))
+
+    e3 = coarse(join3(*take3(1, cps3)))
     x2 = up2(e3, join2(2, cps2h))
     x1 = x1 + prolong(x2[8:56], t1s, p21)
     for _ in range(2):
         x1 = l1.sweep(x1, kg1)
-    tot2 = sum_end(sums2, 1)
-    c4 = pick(tot2, 0) * inv
-    p5r = pick(tot2, 1)
-    x1 = x1 + c4 * x1r
-    tot3 = sum_end(sums3, 2)
-    c5 = (tot3[:, 0:1] + c4 * p5r) * inv
-    x1 = x1 + c5 * w1
+    tot = sum_end(sums2, 1)
+    b4, b41, b42, b43, b5, b51, b52, b53, b54 = (pick(tot, n) for n in range(9))
+    c4 = with_constants(b4, (b41, b42, b43)) * inv
+    c5 = (with_constants(b5, (b51, b52, b53)) + c4 * b54) * inv
+    x1 = (x1 + c4 * x1r) + c5 * w1
 
     for t in range(2):
         y = mm(x1[:, 128 * t : 128 * t + 128], p21[...])
@@ -641,13 +688,13 @@
         + [v((16, 128), F32)] * 2
         + [v((2, 16, 128), F32)]
         + [v((4, 8, 32, 128), F32), v((4, 32, 128), F32)]
-        + [v((3, 8, 24, 128), F32), v((3, 32, 128), F32)]
-        + [v((3, 2, 1, 128), F32), v((3, 15, 1, 128), F32), v((3, 15, 1, 128), F32)]
+        + [v((7, 8, 8, 128), F32), v((7, 32, 128), F32), v((7, 2, 8, 128), F32)]
+        + [v((2, 2, 1, 128), F32), v((2, 15, 1, 128), F32), v((2, 15, 1, 128), F32)]
         + [dma((2, 8))] * 2
         + [dma((10,))] * 4
         + [dma((4, 8))] * 2
-        + [dma((3, 8))] * 2
-        + [dma((3, 2, 15))] * 2
+        + [dma((7, 8))] * 2
+        + [dma((2, 2, 15))] * 2
         + [dma((2,))]
     )
     shape = jax.ShapeDtypeStruct((128, 256), F32)

time: 55 us -> 50.4 us (0.916)
  Pallas kernels: 51.1 us -> 46.5 us
    pallas_call x1, Pallas kernels: 51.1 us -> 46.5 us  [body(): pl.pallas_call(kernel, out_shape=(shape, shape), in_specs=[pl.BlockSpec(m...]
where the time goes in v3:
time: 50.4 us; the launch traced here: 50.3 us
  Pallas kernels  46.5 us (92%)
  local copies, waits for them, and re-layouts  3.11 us (6%)
  between operations  0.65 us (1%)
    pallas_call x1, Pallas kernels, body(): pl.pallas_call(kernel, out_shape=(shape, shape), in_specs=[pl.BlockSpec(m...  46.5 us
    unnamed x6, local copies, waits for them, and re-layouts  3.11 us

profile of v3, /device:TPU:1, one launch (start us, length us, event | category | flops | bytes accessed | tf_op | source)
XLA Modules:
  0.0 50.3 jit_solution(16324506265899313234)
XLA Ops:
  0.6 0.0 copy-start
  0.6 0.9 %copy-done = f32[128,256]{1,0:T(8,128)S(1)} copy-done((f32[128,256]{1,0:T(8,128)S(1)}, f32[128,256]{1,0:T(8,128)}, u32[]{:S(2)}) %copy-start) | copy-done | bytes 131096
  1.5 0.0 copy-start.1
  1.5 0.9 %copy-done.1 = f32[128,256]{1,0:T(8,128)S(1)} copy-done((f32[128,256]{1,0:T(8,128)S(1)}, f32[128,256]{1,0:T(8,128)}, u32[]{:S(2)}) %copy-start.1) | copy-done | bytes 131096
  2.4 46.5 %fcycle.1 = (f32[128,256]{1,0:T(8,128)S(1)}, f32[128,256]{1,0:T(8,128)S(1)}) custom-call(f32[128,256]{1,0:T(8,128)S(1)} %copy-done, f32[128,256]{1,0:T(8,128)S(1)} %copy-done.1), custom_call_target="tpu_custom_call" | custom-call | tf_op jit(solution)/shard_map/fcycle/pallas_call | solution.py:702
  48.9 0.7 %copy.6 = f32[128,256]{1,0:T(8,128)} copy(f32[128,256]{1,0:T(8,128)S(1)} %get-tuple-element.4) | data formatting | bytes 262144
  49.6 0.7 %copy.7 = f32[128,256]{1,0:T(8,128)} copy(f32[128,256]{1,0:T(8,128)S(1)} %get-tuple-element.5) | data formatting | bytes 262144
Async XLA Ops:
  0.6 0.9 %copy-start = (f32[128,256]{1,0:T(8,128)S(1)}, f32[128,256]{1,0:T(8,128)}, u32[]{:S(2)}) copy-start(f32[128,256]{1,0:T(8,128)} %rhs_in.1) | copy-start | bytes 393220
  1.5 0.9 %copy-start.1 = (f32[128,256]{1,0:T(8,128)S(1)}, f32[128,256]{1,0:T(8,128)}, u32[]{:S(2)}) copy-start(f32[128,256]{1,0:T(8,128)} %shf_in.1) | copy-start | bytes 393220

commit v4 on v3

--- a/solution.py
+++ b/solution.py
@@ -104,7 +104,7 @@
     s_side, s_line, g_side, g_line, own3, own3g, ownb,
     x2b, own2, x3b, own3n, own3p,
     ar_in, ar_a, ar_b,
-    e0_ss, e0_rs, s_ss, s_rs, g_ss, g_rs, x2_ss, x2_rs, x3_ss, x3_rs, ar_ss, ar_rs, in_s,
+    rows_of, all_sent, got_border, got_s, got_g, got_2, got_3, got_sum, in_s,
 ):
     gx = lax.axis_index("gx")
     gy = lax.axis_index("gy")
@@ -137,21 +137,25 @@
     in_shf.start()
     in_rhs.start()
 
-    sent = []
+    sent = [0]
     turn = [0]
+
+    def got(sem, rows):
+        ref = rows_of.at[0:rows]
+        pltpu.make_async_copy(ref, ref, sem).wait()
 
     def scratch(pool):
         turn[0] += 1
         return pool.at[turn[0] % pool.shape[0]]
 
-    def send(src, dst, ss, rs, dev):
-        cp = pltpu.make_async_remote_copy(
-            src_ref=src, dst_ref=dst, send_sem=ss, recv_sem=rs,
+    def send(src, dst, sem, dev):
+        pltpu.make_async_remote_copy(
+            src_ref=src, dst_ref=dst, send_sem=all_sent.at[0], recv_sem=sem,
             device_id=dev, device_id_type=MESH,
-        )
-        cp.start()
-        sent.append(cp)
-        return cp
+        ).start()
+        size = src.shape[0] * src.shape[1] // 128
+        sent[0] += size
+        return size
 
     i, j = iota((256, 128), 0), iota((256, 128), 1)
     rm[...] = jnp.where((i >> 1) == j, 0.25, 0.0).astype(BF16)
@@ -219,29 +223,24 @@
 
     ROWS = {-1: (0, 24, 160, 184), 1: (104, 128, 8, 32), 0: (0, 128, 32, 160)}
     COLS = {-1: (0, 128, 384, 512), 1: (128, 256, 0, 128), 0: (0, 256, 128, 384)}
-    first = []
 
     def border(f):
         src, dst = (shf, xs) if f else (rhs, xg)
-        for n, (dz, dy) in enumerate(AROUND):
+        rows = 0
+        for dz, dy in AROUND:
             a, b, c, d = ROWS[dz]
             e, g, h, k = COLS[dy]
-            first.append(
-                send(
-                    src.at[a:b, e:g], dst.at[8 + c : 8 + d, h:k],
-                    e0_ss.at[f, n], e0_rs.at[f, n], near(dz, dy),
-                )
+            rows += send(
+                src.at[a:b, e:g], dst.at[8 + c : 8 + d, h:k], got_border.at[f], near(dz, dy)
             )
-
-    def side_send(src, buf, ss, rs):
-        return [
-            send(src, buf.at[n], ss.at[n], rs.at[n], near(0, d))
-            for n, d in enumerate(SIDE)
-        ]
-
-    def side_join(own, buf, cps):
-        for cp in cps:
-            cp.wait_recv()
+        return rows
+
+    def side_send(src, buf, sem):
+        for n, d in enumerate(SIDE):
+            send(src, buf.at[n], sem.at[0], near(0, d))
+
+    def side_join(own, buf, sem):
+        got(sem.at[0], 64)
         right1, left1, right2, left2 = (buf[n] for n in range(4))
         lane = iota((16, 128), 1)
         out = jnp.where(lane < 48, pltpu.roll(left1, 96, axis=1), own)
@@ -249,39 +248,25 @@
         out = jnp.where(lane >= 80, pltpu.roll(right1, 32, axis=1), out)
         return jnp.where(lane >= 112, pltpu.roll(right2, 64, axis=1), out)
 
-    def line_send(src, buf, ss, rs):
-        return [
-            send(
-                src, buf.at[16 * (3 - d) : 16 * (4 - d)],
-                ss.at[4 + n], rs.at[4 + n], near(d, 0),
-            )
-            for n, d in enumerate(LINE)
-        ]
+    def line_send(src, buf, sem):
+        for d in LINE:
+            send(src, buf.at[16 * (3 - d) : 16 * (4 - d)], sem.at[1], near(d, 0))
 
     SRC2 = {-1: (0, 16), 1: (16, 32), 0: (0, 32)}
 
     def send2(x, k):
         own2[k] = x
-        src, buf = own2.at[k], x2b.at[k]
-        cps = []
         for n, (dz, dy) in enumerate(AROUND):
             a, b = SRC2[dz]
-            cps.append(
-                send(
-                    src.at[a:b], buf.at[n, 0 : b - a],
-                    x2_ss.at[k, n], x2_rs.at[k, n], near(dz, dy),
-                )
-            )
-        return cps
+            send(own2.at[k, a:b], x2b.at[k, n, 0 : b - a], got_2.at[k], near(dz, dy))
 
     def lanes3(left, mid, right, lo, hi, move):
         lane = iota(mid.shape, 1)
         out = jnp.where(lane < lo, pltpu.roll(left, 128 - move, axis=1), mid)
         return jnp.where(lane >= hi, pltpu.roll(right, move, axis=1), out)
 
-    def join2(k, cps):
-        for cp in cps:
-            cp.wait_recv()
+    def join2(k):
+        got(got_2.at[k], 6 * 16 + 2 * 32)
         own, buf = own2[k], x2b.at[k]
         dn, up, rt, lf, dr, dl, ur, ul = range(8)
         return jnp.concatenate(
@@ -303,17 +288,11 @@
         own3n[k] = x
         own3p[k, 0] = pack3(x, 8)
         own3p[k, 1] = pack3(x, 0)
-        return [
-            send(
-                own3p.at[k, 1 if dz == 1 else 0], x3b.at[k, n],
-                x3_ss.at[k, n], x3_rs.at[k, n], near(dz, dy),
-            )
-            for n, (dz, dy) in enumerate(AROUND)
-        ]
-
-    def take3(k, cps):
-        for cp in cps:
-            cp.wait_recv()
+        for n, (dz, dy) in enumerate(AROUND):
+            send(own3p.at[k, 1 if dz == 1 else 0], x3b.at[k, n], got_3.at[k], near(dz, dy))
+
+    def take3(k):
+        got(got_3.at[k], 64)
         return [own3n[k, 8:24]] + [x3b[k, n] for n in range(8)]
 
     def join3(own, dn, up, rt, lf, dr, dl, ur, ul):
@@ -333,45 +312,31 @@
 
     def sum_start(row, k):
         ar_in[k, 0] = row
-        return [
-            send(
-                ar_in.at[k, 0], ar_a.at[k, n],
-                ar_ss.at[k, 0, n], ar_rs.at[k, 0, n], in_a(*o),
-            )
-            for n, o in enumerate(GROUP_A)
-        ]
-
-    def sum_next(cps, k):
-        for cp in cps:
-            cp.wait_recv()
-        part = ar_in[k, 0] + jnp.sum(ar_a[k], axis=0)
-        ar_in[k, 1] = part
-        return [
-            send(
-                ar_in.at[k, 1], ar_b.at[k, n],
-                ar_ss.at[k, 1, n], ar_rs.at[k, 1, n], in_b(*o),
-            )
-            for n, o in enumerate(GROUP_B)
-        ]
-
-    def sum_end(cps, k):
-        for cp in cps:
-            cp.wait_recv()
+        for n, o in enumerate(GROUP_A):
+            send(ar_in.at[k, 0], ar_a.at[k, n], got_sum.at[k, 0], in_a(*o))
+
+    def sum_next(k):
+        got(got_sum.at[k, 0], 15)
+        ar_in[k, 1] = ar_in[k, 0] + jnp.sum(ar_a[k], axis=0)
+        for n, o in enumerate(GROUP_B):
+            send(ar_in.at[k, 1], ar_b.at[k, n], got_sum.at[k, 1], in_b(*o))
+
+    def sum_end(k):
+        got(got_sum.at[k, 1], 15)
         return ar_in[k, 1] + jnp.sum(ar_b[k], axis=0)
 
-    side_s = side_send(own3, s_side, s_ss, s_rs)
-    border(1)
+    side_send(own3, s_side, got_s)
+    border_rows = border(1)
     border(0)
-    cps2s = send2(own2[0], 0)
-    s_row = side_join(own3[...], s_side, side_s)
+    send2(own2[0], 0)
+    s_row = side_join(own3[...], s_side, got_s)
     ownb[0] = s_row
-    line_s = line_send(ownb.at[0], s_line, s_ss, s_rs)
+    line_send(ownb.at[0], s_line, got_s)
     s_line[48:64] = s_row
 
     row0 = gx * 128 - 32
     col0 = gy * 256 - 128
-    for cp in first[:8]:
-        cp.wait_recv()
+    got(got_border.at[1], border_rows)
     STEP = 16
 
     def near4(ref, r, n=STEP):
@@ -400,8 +365,7 @@
     s2 = restrict(s1, t1s, rm)
     l2a = Level(2, s2, gx * 32 - 8, gy * 64 - 32)
 
-    for cp in first[8:]:
-        cp.wait_recv()
+    got(got_border.at[0], border_rows)
     for r in range(0, 192, STEP):
         w = slice(8 + r, 8 + r + STEP)
         kg0[w, :] = kk[w, :] * xg[w, :]
@@ -425,11 +389,10 @@
     g3 = restrict(r2, t2s, r23)
     g3own = g3[4:20]
     own3g[...] = g3own
-    side_g = side_send(own3g, g_side, g_ss, g_rs)
-    cps2g = send2(g2[8:40], 1)
-
-    for cp in line_s:
-        cp.wait_recv()
+    side_send(own3g, g_side, got_g)
+    send2(g2[8:40], 1)
+
+    got(got_s.at[1], 96)
     l3 = Level(3, s_line[...], gx * 16 - 48, gy * 32 - 48)
     s4 = restrict(s_line[...], t3s, r34)
     l4 = Level(4, s4, gx * 8 - 24, gy * 16 - 24, iota((56, 128), 1) < 64)
@@ -471,11 +434,11 @@
     row = jnp.zeros((1, 128), F32)
     for n, p in enumerate(parts):
         row = jnp.where(lane == n, p, row)
-    sums1 = sum_start(row, 0)
-
-    g_row = side_join(g3own, g_side, side_g)
+    sum_start(row, 0)
+
+    g_row = side_join(g3own, g_side, got_g)
     ownb[1] = g_row
-    line_g = line_send(ownb.at[1], g_line, g_ss, g_rs)
+    line_send(ownb.at[1], g_line, got_g)
     g_line[48:64] = g_row
 
     def coarse(G):
@@ -531,32 +494,32 @@
     for _ in range(2):
         ra, rb = l3.sweep0(ra), l3.sweep0(rb)
 
-    s2w = join2(0, cps2s)
+    s2w = join2(0)
     l2 = Level(2, s2w, gx * 32 - 16, gy * 64 - 32)
     start2 = [prolong(r[40:72], t2s, p32) for r in (ra, rb, f2)]
     after2 = start2
     for _ in range(4):
         after2 = [l2.sweep0(x) for x in after2]
     h_of = [restrict(-l2.apply(x), t2s, r23) for x in after2]
-    cps_of = [send3(h, 3 + n) for n, h in enumerate(h_of)]
+    for n, h in enumerate(h_of):
+        send3(h, 3 + n)
     y2 = l2.sweep0(l2.sweep0(prolong(y3[40:72], t2s, p32)))
     f5 = l1.sweep0(l1.sweep0(prolong(y2[8:56], t1s, p21)))
     f5 = l1.sweep0(l1.sweep0(f5)) * (1.0 / 64)
     ga, va, ta, ha = down2(4.0 * restrict(l1.apply(f5), t1s, rm))
     ha = 4.0 * ha
-    cpsa = send3(ha, 6)
+    send3(ha, 6)
     f4 = l2.sweep0(l2.sweep0(y2)) * (1.0 / 16)
     p4_of = [-dot2(f4, l2.apply(x)) for x in start2]
     p54 = -dot3(ha[8:24], f2[48:64])
 
-    sums1 = sum_next(sums1, 0)
-
-    g2w = join2(1, cps2g)
+    sum_next(0)
+
+    g2w = join2(1)
     kg2 = l2.k * g2w
     v2 = l2.sweep(kg2, kg2)
     pv = dot1(f5, l1.residual(v1, g1)) - dot2(va, g2w)
-    for cp in line_g:
-        cp.wait_recv()
+    got(got_g.at[1], 96)
     G3 = g_line[...]
     kg3 = l3.k * G3
     v3 = l3.sweep(kg3, kg3)
@@ -580,8 +543,8 @@
     for _ in range(4):
         x2 = l2.sweep(x2, kg2)
     g3 = restrict(l2.residual(x2, g2w), t2s, r23)
-    cps3 = send3(g3, 0)
-    ma = coarse(join3(*take3(6, cpsa)))[8:24]
+    send3(g3, 0)
+    ma = coarse(join3(*take3(6)))[8:24]
     p5 = pv - dot2(ta, x2) - dot3(ma, g3[8:24])
     p5_of = [
         -dot2(ta, x) - dot3(ma, h[8:24]) for x, h in zip(after2, h_of)
@@ -589,17 +552,17 @@
     row = jnp.zeros((1, 128), F32)
     for n, p in enumerate([p4, *p4_of, p5, *p5_of, p54]):
         row = jnp.where(lane == n, p, row)
-    sums2 = sum_start(row, 1)
+    sum_start(row, 1)
+    tot = sum_end(0)
 
     z2 = l2.sweep0(l2.sweep0(prolong(f2[40:72], t2s, p32)))
     z1 = prolong(z2[8:56], t1s, p21)
     w1 = l1.sweep0(l1.sweep0(z1))
     d1 = l1.sweep0(l1.sweep0(w1))
     h2, _, _, h3 = down2(restrict(-l1.apply(d1), t1s, rm))
-    cps3r = send3(h3, 2)
-    cps2r = send2(h2[16:48], 3)
-
-    tot = sum_end(sums1, 0)
+    send3(h3, 2)
+    send2(h2[16:48], 3)
+
     a1, a2, a3, ones_total, w6_total, qw12, qw6 = (pick(tot, n) for n in range(7))
     inv = 1.0 / ones_total
     c1 = a1 * inv
@@ -610,8 +573,8 @@
         return ((x + c1 * parts[0]) + c2 * parts[1]) + c3 * parts[2]
 
     x2 = with_constants(x2, after2)
-    parts = [take3(3 + n, cps) for n, cps in enumerate(cps_of)]
-    G = [with_constants(b, p) for b, p in zip(take3(0, cps3), zip(*parts))]
+    parts = [take3(3 + n) for n in range(3)]
+    G = [with_constants(b, p) for b, p in zip(take3(0), zip(*parts))]
     x2 = x2 + prolong(coarse(join3(*G)), t2s, p32)
     for _ in range(2):
         x2 = l2.sweep(x2, kg2)
@@ -620,19 +583,19 @@
     for _ in range(4):
         x1 = l1.sweep(x1, kg1)
     g2, _, _, g3 = down2(restrict(l1.residual(x1, g1), t1s, rm))
-    cps3 = send3(g3, 1)
-    cps2h = send2(g2[16:48], 2)
-    sums2 = sum_next(sums2, 1)
-    e3 = coarse(join3(*take3(2, cps3r)))
-    x2r = up2(e3, join2(3, cps2r))
+    send3(g3, 1)
+    send2(g2[16:48], 2)
+    sum_next(1)
+    e3 = coarse(join3(*take3(2)))
+    x2r = up2(e3, join2(3))
     x1r = l1.sweep0(l1.sweep0(d1 + prolong(x2r[8:56], t1s, p21)))
 
-    e3 = coarse(join3(*take3(1, cps3)))
-    x2 = up2(e3, join2(2, cps2h))
+    e3 = coarse(join3(*take3(1)))
+    x2 = up2(e3, join2(2))
     x1 = x1 + prolong(x2[8:56], t1s, p21)
     for _ in range(2):
         x1 = l1.sweep(x1, kg1)
-    tot = sum_end(sums2, 1)
+    tot = sum_end(1)
     b4, b41, b42, b43, b5, b51, b52, b53, b54 = (pick(tot, n) for n in range(9))
     c4 = with_constants(b4, (b41, b42, b43)) * inv
     c5 = (with_constants(b5, (b51, b52, b53)) + c4 * b54) * inv
@@ -659,8 +622,7 @@
         out = rhs[r - 32 : r - 32 + STEP, :] + around[:, 128:384]
         out = out - (4.0 + shf[r - 32 : r - 32 + STEP, :]) * c[:, 128:384]
         res[r - 32 : r - 32 + STEP, :] = out
-    for cp in sent:
-        cp.wait_send()
+    got(all_sent.at[0], sent[0])
 
 
 def tmp0_pair(ref, t, rows):
@@ -690,12 +652,8 @@
         + [v((4, 8, 32, 128), F32), v((4, 32, 128), F32)]
         + [v((7, 8, 8, 128), F32), v((7, 32, 128), F32), v((7, 2, 8, 128), F32)]
         + [v((2, 2, 1, 128), F32), v((2, 15, 1, 128), F32), v((2, 15, 1, 128), F32)]
-        + [dma((2, 8))] * 2
-        + [dma((10,))] * 4
-        + [dma((4, 8))] * 2
-        + [dma((7, 8))] * 2
-        + [dma((2, 2, 15))] * 2
-        + [dma((2,))]
+        + [v((4096, 128), F32)]
+        + [dma((1,)), dma((2,)), dma((2,)), dma((2,)), dma((4,)), dma((7,)), dma((2, 2)), dma((2,))]
     )
     shape = jax.ShapeDtypeStruct((128, 256), F32)
     vm = pl.BlockSpec(memory_space=pltpu.VMEM)

time: 50.4 us -> 46.9 us (0.931)
  Pallas kernels: 46.5 us -> 43 us
    pallas_call x1, Pallas kernels: 46.5 us -> 43 us  [body(): pl.pallas_call(kernel, out_shape=(shape, shape), in_specs=[pl.BlockSpec(m...]
where the time goes in v4:
time: 46.9 us; the launch traced here: 46.8 us
  Pallas kernels  43 us (92%)
  local copies, waits for them, and re-layouts  3.11 us (7%)
  between operations  0.65 us (1%)
    pallas_call x1, Pallas kernels, body(): pl.pallas_call(kernel, out_shape=(shape, shape), in_specs=[pl.BlockSpec(m...  43 us
    unnamed x6, local copies, waits for them, and re-layouts  3.11 us

profile of v4, /device:TPU:1, one launch (start us, length us, event | category | flops | bytes accessed | tf_op | source)
XLA Modules:
  0.0 46.8 jit_solution(15068175542744136861)
XLA Ops:
  0.6 0.0 copy-start
  0.6 0.9 %copy-done = f32[128,256]{1,0:T(8,128)S(1)} copy-done((f32[128,256]{1,0:T(8,128)S(1)}, f32[128,256]{1,0:T(8,128)}, u32[]{:S(2)}) %copy-start) | copy-done | bytes 131096
  1.5 0.0 copy-start.1
  1.5 0.9 %copy-done.1 = f32[128,256]{1,0:T(8,128)S(1)} copy-done((f32[128,256]{1,0:T(8,128)S(1)}, f32[128,256]{1,0:T(8,128)}, u32[]{:S(2)}) %copy-start.1) | copy-done | bytes 131096
  2.4 43.0 %fcycle.1 = (f32[128,256]{1,0:T(8,128)S(1)}, f32[128,256]{1,0:T(8,128)S(1)}) custom-call(f32[128,256]{1,0:T(8,128)S(1)} %copy-done, f32[128,256]{1,0:T(8,128)S(1)} %copy-done.1), custom_call_target="tpu_custom_call" | custom-call | tf_op jit(solution)/shard_map/fcycle/pallas_call | solution.py:660
  45.4 0.7 %copy.6 = f32[128,256]{1,0:T(8,128)} copy(f32[128,256]{1,0:T(8,128)S(1)} %get-tuple-element.4) | data formatting | bytes 262144
  46.1 0.7 %copy.7 = f32[128,256]{1,0:T(8,128)} copy(f32[128,256]{1,0:T(8,128)S(1)} %get-tuple-element.5) | data formatting | bytes 262144
Async XLA Ops:
  0.6 0.9 %copy-start = (f32[128,256]{1,0:T(8,128)S(1)}, f32[128,256]{1,0:T(8,128)}, u32[]{:S(2)}) copy-start(f32[128,256]{1,0:T(8,128)} %rhs_in.1) | copy-start | bytes 393220
  1.5 0.9 %copy-start.1 = (f32[128,256]{1,0:T(8,128)S(1)}, f32[128,256]{1,0:T(8,128)}, u32[]{:S(2)}) copy-start(f32[128,256]{1,0:T(8,128)} %shf_in.1) | copy-start | bytes 393220

commit v5 on v4

--- a/solution.py
+++ b/solution.py
@@ -14,8 +14,11 @@
 LV_D = [4.0 ** (1 - l) for l in range(5)]
 
 AROUND = [(-1, 0), (1, 0), (0, -1), (0, 1), (-1, -1), (-1, 1), (1, -1), (1, 1)]
+MIRROR = [1, 0, 3, 2, 7, 6, 5, 4]
 SIDE = [-1, 1, -2, 2]
 LINE = [-1, 1, -2, 2, -3, 3]
+P1, P2, P3, P4 = (1, 1), (2,), (2,), (2,)
+PR, P3B, P4B = (1, 1), (2,), (3, 2)
 GROUP_A = [(dz, dc) for dz in range(8) for dc in range(2) if dz or dc]
 GROUP_B = [(dy, dx) for dy in range(4) for dx in range(4) if dy or dx]
 
@@ -24,14 +27,35 @@
     return lax.broadcasted_iota(jnp.int32, shape, dim)
 
 
+def shifted(v, by):
+    by %= v.shape[1]
+    return pltpu.roll(v, by, axis=1) if by else v
+
+
+def updown(v):
+    return pltpu.roll(v, 1, axis=0) + pltpu.roll(v, v.shape[0] - 1, axis=0)
+
+
 def beside(v):
-    r, c = v.shape
-    return (
-        pltpu.roll(v, 1, axis=0)
-        + pltpu.roll(v, r - 1, axis=0)
-        + pltpu.roll(v, 1, axis=1)
-        + pltpu.roll(v, c - 1, axis=1)
-    )
+    return updown(v) + (shifted(v, 1) + shifted(v, -1))
+
+
+class Moved:
+    def __init__(self, x):
+        self.at = {0: x}
+
+    def __call__(self, by):
+        if by not in self.at:
+            self.at[by] = shifted(self.at[0], by)
+        return self.at[by]
+
+
+class MovedRows:
+    def __init__(self, of, lo, hi):
+        self.of, self.lo, self.hi = of, lo, hi
+
+    def __call__(self, by):
+        return self.of(by)[self.lo : self.hi]
 
 
 def inside(shape, level, row0, col0):
@@ -51,24 +75,39 @@
             ok = ok & mask
         self.ok = ok
         self.k = jnp.where(ok, 0.8 / self.d, 0.0)
-        self.km = self.k * LV_Q[level]
+        self.km = Moved(self.k * LV_Q[level])
 
     def cut(self, lo, hi):
         out = object.__new__(Level)
-        out.level = self.level
-        out.d, out.k, out.km, out.ok = (
-            self.d[lo:hi],
-            self.k[lo:hi],
-            self.km[lo:hi],
-            None,
-        )
+        out.level, out.ok = self.level, None
+        out.d, out.k = self.d[lo:hi], self.k[lo:hi]
+        out.km = MovedRows(self.km, lo, hi)
         return out
 
-    def sweep0(self, v):
-        return 0.2 * v + self.km * beside(v)
-
-    def sweep(self, v, kg):
-        return 0.2 * v + kg + self.km * beside(v)
+    def sweeps(self, v, kg, plan):
+        for n in plan:
+            v = self.several(v, kg, n)
+        return v
+
+    def several(self, v, kg, n):
+        v = v if isinstance(v, Moved) else Moved(v)
+        x = {s: v(s) for s in range(-n, n + 1)}
+        for t in range(n - 1, -1, -1):
+            x = {s: self.once(x, kg, s) for s in range(-t, t + 1)}
+            if t == 0:
+                return x[0]
+
+    def once(self, x, kg, s):
+        out = 0.2 * x[s] if kg is None else 0.2 * x[s] + kg(s)
+        return out + self.km(s) * (updown(x[s]) + (x[s - 1] + x[s + 1]))
+
+    def down(self, g):
+        kg = Moved(self.k * g)
+        x = {s: kg(s) for s in range(-2, 3)}
+        x = {s: self.once(x, kg, s) for s in range(-1, 2)}
+        v = x[0]
+        r = g - self.d * v + LV_Q[self.level] * (updown(v) + (x[1] + x[-1]))
+        return kg, v, r
 
     def residual(self, v, g):
         return g - self.d * v + LV_Q[self.level] * beside(v)
@@ -104,7 +143,7 @@
     s_side, s_line, g_side, g_line, own3, own3g, ownb,
     x2b, own2, x3b, own3n, own3p,
     ar_in, ar_a, ar_b,
-    rows_of, all_sent, got_border, got_s, got_g, got_2, got_3, got_sum, in_s,
+    edge_out, edge_in, corner_out, corner_in, rows_of, all_sent, got_border, got_s, got_g, got_2, got_3, got_sum, in_s,
 ):
     gx = lax.axis_index("gx")
     gy = lax.axis_index("gy")
@@ -112,8 +151,33 @@
     quad = lax.div(gy, 2)
     qy, qx = lax.div(quad, 4), lax.rem(quad, 4)
 
-    def near(dz, dy):
-        return (lax.rem(gx + (dz + GX), GX), lax.rem(gy + (dy + GY), GY))
+    def past(at, by, size):
+        if by > 0:
+            return lax.div(at + by, size)
+        return 1 - lax.div(at + (by + size), size) if by < 0 else 0 * at
+
+    other_core = gy + 1 - 2 * core
+    other_row = gx + 1 - 2 * lax.rem(gx, 2)
+
+    def beyond(dz, dy):
+        if not dy:
+            out = past(gx, dz, GX)
+            return (gx + (1 - out) * dz, gy + out * (other_core - gy)), out
+        if not dz:
+            out = past(gy, dy, GY)
+            return (gx + out * (other_row - gx), gy + (1 - out) * dy), out
+        zo, yo = past(gx, dz, GX), past(gy, dy, GY)
+        high = lax.div(gx, 4)
+        if dz > 0:
+            ring = (1 - high) * other_row + high * (4 + lax.rem(gx, 3))
+        else:
+            ring = high * other_row + (1 - high) * (1 + lax.rem(gx, 3))
+        to_z = zo * gx + (1 - zo) * (yo * ring + (1 - yo) * (gx + dz))
+        to_y = zo * other_core + (1 - zo) * (yo * gy + (1 - yo) * (gy + dy))
+        return (to_z, to_y), zo + (1 - zo) * yo
+
+    def slot(n, mirror, out):
+        return n + out * (mirror - n)
 
     def in_a(dz, dc):
         return (lax.rem(gx + dz, GX), gy - core + lax.rem(core + dc, 2))
@@ -123,7 +187,7 @@
 
     barrier = pltpu.get_barrier_semaphore()
     partners = (
-        [near(*o) for o in AROUND]
+        [beyond(*o)[0] for o in AROUND]
         + [in_a(*o) for o in GROUP_A]
         + [in_b(*o) for o in GROUP_B]
     )
@@ -219,25 +283,73 @@
     own2[0] = pltpu.roll(restrict(s1own, t1s, r34), 32, axis=1)
     in_rhs.wait()
 
+    def pack_border(f, x):
+        for side in range(2):
+            e = x[:, 128 * side : 128 * side + 128]
+            at = 96 * side
+            lane = iota((32, 128), 1)
+            out = shifted(e[0:32], -at)
+            for n in range(1, 4):
+                out = jnp.where(lane < 32 * n, out, shifted(e[32 * n : 32 * n + 32], 32 * n - at))
+            edge_out[f, side] = out
+            lane = iota((8, 128), 1)
+            for end in range(2):
+                top = 104 * end
+                out = shifted(e[top : top + 8], -at)
+                for n in range(1, 3):
+                    part = e[top + 8 * n : top + 8 * n + 8]
+                    out = jnp.where(lane < 32 * n, out, shifted(part, 32 * n - at))
+                corner_out[f, 2 * end + side] = out
+
+    pack_border(1, s0)
+    pack_border(0, rhs[...])
+
     pl.semaphore_wait(barrier, len(partners))
-
-    ROWS = {-1: (0, 24, 160, 184), 1: (104, 128, 8, 32), 0: (0, 128, 32, 160)}
-    COLS = {-1: (0, 128, 384, 512), 1: (128, 256, 0, 128), 0: (0, 256, 128, 384)}
 
     def border(f):
         src, dst = (shf, xs) if f else (rhs, xg)
+        sem = got_border.at[f]
         rows = 0
-        for dz, dy in AROUND:
-            a, b, c, d = ROWS[dz]
-            e, g, h, k = COLS[dy]
-            rows += send(
-                src.at[a:b, e:g], dst.at[8 + c : 8 + d, h:k], got_border.at[f], near(dz, dy)
-            )
+        for dz, lo, to, mirror in ((-1, 0, 168, 16), (1, 104, 16, 168)):
+            dev, out = beyond(dz, 0)
+            at = pl.ds(pl.multiple_of(slot(to, mirror, out), 8), 24)
+            rows += send(src.at[lo : lo + 24, :], dst.at[at, 128:384], sem, dev)
+        for side in range(2):
+            dy = 2 * side - 1
+            dev, out = beyond(0, dy)
+            rows += send(edge_out.at[f, side], edge_in.at[f, slot(side, 1 - side, out)], sem, dev)
+            for end in range(2):
+                n = 2 * end + side
+                dev, out = beyond(2 * end - 1, dy)
+                rows += send(corner_out.at[f, n], corner_in.at[f, slot(n, 3 - n, out)], sem, dev)
         return rows
+
+    def unpack_border(f):
+        dst = xs if f else xg
+        for side in range(2):
+            lo = 0 if side else 384
+            at = 96 * side
+            lane = iota((32, 128), 1)
+            keep = lane >= 96 if side else lane < 32
+            p = edge_in[f, side]
+            for n in range(4):
+                dst[40 + 32 * n : 72 + 32 * n, lo : lo + 128] = jnp.where(
+                    keep, shifted(p, at - 32 * n), 0.0
+                )
+            lane = iota((8, 128), 1)
+            keep = lane >= 96 if side else lane < 32
+            for end in range(2):
+                top = 16 if end else 168
+                p = corner_in[f, 2 * end + side]
+                for n in range(3):
+                    dst[top + 8 * n : top + 8 * n + 8, lo : lo + 128] = jnp.where(
+                        keep, shifted(p, at - 32 * n), 0.0
+                    )
 
     def side_send(src, buf, sem):
         for n, d in enumerate(SIDE):
-            send(src, buf.at[n], sem.at[0], near(0, d))
+            dev, out = beyond(0, d)
+            send(src, buf.at[slot(n, n ^ 1, out)], sem.at[0], dev)
 
     def side_join(own, buf, sem):
         got(sem.at[0], 64)
@@ -250,7 +362,9 @@
 
     def line_send(src, buf, sem):
         for d in LINE:
-            send(src, buf.at[16 * (3 - d) : 16 * (4 - d)], sem.at[1], near(d, 0))
+            dev, out = beyond(d, 0)
+            at = pl.ds(pl.multiple_of(16 * slot(3 - d, 3 + d, out), 8), 16)
+            send(src, buf.at[at], sem.at[1], dev)
 
     SRC2 = {-1: (0, 16), 1: (16, 32), 0: (0, 32)}
 
@@ -258,7 +372,9 @@
         own2[k] = x
         for n, (dz, dy) in enumerate(AROUND):
             a, b = SRC2[dz]
-            send(own2.at[k, a:b], x2b.at[k, n, 0 : b - a], got_2.at[k], near(dz, dy))
+            dev, out = beyond(dz, dy)
+            at = slot(n, MIRROR[n], out)
+            send(own2.at[k, a:b], x2b.at[k, at, 0 : b - a], got_2.at[k], dev)
 
     def lanes3(left, mid, right, lo, hi, move):
         lane = iota(mid.shape, 1)
@@ -289,7 +405,9 @@
         own3p[k, 0] = pack3(x, 8)
         own3p[k, 1] = pack3(x, 0)
         for n, (dz, dy) in enumerate(AROUND):
-            send(own3p.at[k, 1 if dz == 1 else 0], x3b.at[k, n], got_3.at[k], near(dz, dy))
+            dev, out = beyond(dz, dy)
+            at = slot(n, MIRROR[n], out)
+            send(own3p.at[k, 1 if dz == 1 else 0], x3b.at[k, at], got_3.at[k], dev)
 
     def take3(k):
         got(got_3.at[k], 64)
@@ -337,6 +455,7 @@
     row0 = gx * 128 - 32
     col0 = gy * 256 - 128
     got(got_border.at[1], border_rows)
+    unpack_border(1)
     STEP = 16
 
     def near4(ref, r, n=STEP):
@@ -366,6 +485,7 @@
     l2a = Level(2, s2, gx * 32 - 8, gy * 64 - 32)
 
     got(got_border.at[0], border_rows)
+    unpack_border(0)
     for r in range(0, 192, STEP):
         w = slice(8 + r, 8 + r + STEP)
         kg0[w, :] = kk[w, :] * xg[w, :]
@@ -381,11 +501,9 @@
             tmp0[t, r : r + STEP, :] = out[:, 128 * t : 128 * t + 128]
     g1 = jnp.concatenate([mm(tmp0_pair(tmp0, t, 192), rm[...]) for t in range(2)], axis=1)
 
-    kg1 = l1.k * g1
-    v1 = l1.sweep(kg1, kg1)
-    g2 = restrict(l1.residual(v1, g1), t1s, rm)
-    kg = l2a.k * g2
-    r2 = l2a.residual(l2a.sweep(kg, kg), g2)
+    kg1, v1, r1 = l1.down(g1)
+    g2 = restrict(r1, t1s, rm)
+    _, _, r2 = l2a.down(g2)
     g3 = restrict(r2, t2s, r23)
     g3own = g3[4:20]
     own3g[...] = g3own
@@ -399,21 +517,15 @@
 
     one4 = jnp.where(l4.ok, 1.0, 0.0)
     one3 = jnp.where(l3.ok, 1.0, 0.0)
-    w6 = one4
-    for _ in range(6):
-        w6 = l4.sweep0(w6)
-    w12 = w6
-    for _ in range(6):
-        w12 = l4.sweep0(w12)
-    y3 = l3.sweep0(l3.sweep0(one3))
-    u = l3.sweep0(l3.sweep0(y3))
+    w6 = l4.sweeps(one4, None, P4 * 3)
+    w12 = l4.sweeps(w6, None, P4 * 3)
+    y3 = l3.sweeps(one3, None, P3)
+    u = l3.sweeps(y3, None, P3)
     q = 4.0 * restrict(jnp.where(l3.ok, l3.apply(u), 0.0), t3s, r34)
-    kq = l4.k * q
-    z = kq
-    for _ in range(11):
-        z = l4.sweep(z, kq)
-    f3 = l3.sweep0(l3.sweep0(u - 0.25 * prolong(z, t3s, p43)))
-    f2 = l3.sweep0(l3.sweep0(prolong(w6, t3s, p43)))
+    kq = Moved(l4.k * q)
+    z = l4.sweeps(kq, kq, P4 * 5 + (1,))
+    f3 = l3.sweeps(u - 0.25 * prolong(z, t3s, p43), None, P3)
+    f2 = l3.sweeps(prolong(w6, t3s, p43), None, P3)
     lane3 = (iota((16, 128), 1) >= 48) & (iota((16, 128), 1) < 80)
     lane4 = (iota((8, 128), 1) >= 24) & (iota((8, 128), 1) < 40)
     g3m = jnp.where(lane3, g3own, 0.0)
@@ -436,112 +548,89 @@
         row = jnp.where(lane == n, p, row)
     sum_start(row, 0)
 
+    def coarse(G):
+        kgc, v, r = l3b.down(G)
+        kgd = Moved(l4b.k * restrict(r, t3s, r34))
+        e = l4b.sweeps(kgd, kgd, P4B)
+        return l3b.sweeps(v + prolong(e, t3s, p43), kgc, P3B)[16:48]
+
+    def down2(x):
+        pad = jnp.zeros((8, 128), F32)
+        g = jnp.concatenate([pad, x, pad], axis=0)
+        kg, v, r = l2.down(g)
+        return g, v, r, restrict(r, t2s, r23)
+
+    def up2(e3, g):
+        kg, v, _ = l2.down(g)
+        return l2.sweeps(v + prolong(e3, t2s, p32), kg, P2)
+
+    l3b = l3.cut(24, 88)
+    l4b = l4.cut(12, 44)
+    lane1 = (iota((64, 256), 1) >= 64) & (iota((64, 256), 1) < 192)
+    lane2 = (iota((32, 128), 1) >= 32) & (iota((32, 128), 1) < 96)
+
+    def dot1(a, b):
+        return total(jnp.where(lane1, a[16:80] * b[16:80], 0.0))
+
+    def dot2(a, b):
+        return total(jnp.where(lane2, a[16:48] * b[16:48], 0.0))
+
+    def dot3(a, b):
+        return total(jnp.where(lane3, a * b, 0.0))
+
+    s2w = join2(0)
+    l2 = Level(2, s2w, gx * 32 - 16, gy * 64 - 32)
+    y2 = l2.sweeps(prolong(y3[40:72], t2s, p32), None, P2)
+    f5 = l1.sweeps(prolong(y2[8:56], t1s, p21), None, P1 * 2) * (1.0 / 64)
+    ga, va, ta, ha = down2(4.0 * restrict(l1.apply(f5), t1s, rm))
+    ha = 4.0 * ha
+    send3(ha, 6)
+
     g_row = side_join(g3own, g_side, got_g)
     ownb[1] = g_row
     line_send(ownb.at[1], g_line, got_g)
     g_line[48:64] = g_row
 
-    def coarse(G):
-        kgc = l3b.k * G
-        v = l3b.sweep(kgc, kgc)
-        kgd = l4b.k * restrict(l3b.residual(v, G), t3s, r34)
-        e = kgd
-        for _ in range(5):
-            e = l4b.sweep(e, kgd)
-        x = v + prolong(e, t3s, p43)
-        for _ in range(2):
-            x = l3b.sweep(x, kgc)
-        return x[16:48]
-
-    def down2(x):
-        pad = jnp.zeros((8, 128), F32)
-        g = jnp.concatenate([pad, x, pad], axis=0)
-        kg = l2.k * g
-        v = l2.sweep(kg, kg)
-        r = l2.residual(v, g)
-        return g, v, r, restrict(r, t2s, r23)
-
-    def up2(e3, g):
-        kg = l2.k * g
-        x = l2.sweep(kg, kg) + prolong(e3, t2s, p32)
-        for _ in range(2):
-            x = l2.sweep(x, kg)
-        return x
-
-    l3b = l3.cut(24, 88)
-    l4b = l4.cut(12, 44)
-    lane1 = (iota((64, 256), 1) >= 64) & (iota((64, 256), 1) < 192)
-    lane2 = (iota((32, 128), 1) >= 32) & (iota((32, 128), 1) < 96)
-
-    def dot1(a, b):
-        return total(jnp.where(lane1, a[16:80] * b[16:80], 0.0))
-
-    def dot2(a, b):
-        return total(jnp.where(lane2, a[16:48] * b[16:48], 0.0))
-
-    def dot3(a, b):
-        return total(jnp.where(lane3, a * b, 0.0))
-
     ra, rb = prolong(w12, t3s, p43), prolong(w6, t3s, p43)
-    for _ in range(4):
-        ra, rb = l3.sweep0(ra), l3.sweep0(rb)
-    ka = l4.k * restrict(-l3.apply(ra), t3s, r34)
-    kb = l4.k * restrict(-l3.apply(rb), t3s, r34)
-    ea, eb = ka, kb
-    for _ in range(5):
-        ea, eb = l4.sweep(ea, ka), l4.sweep(eb, kb)
+    ra, rb = (l3.sweeps(x, None, PR * 2) for x in (ra, rb))
+    ka, kb = (Moved(l4.k * restrict(-l3.apply(x), t3s, r34)) for x in (ra, rb))
+    ea, eb = (l4.sweeps(x, x, P4 * 2 + (1,)) for x in (ka, kb))
     ra, rb = ra + prolong(ea, t3s, p43), rb + prolong(eb, t3s, p43)
-    for _ in range(2):
-        ra, rb = l3.sweep0(ra), l3.sweep0(rb)
-
-    s2w = join2(0)
-    l2 = Level(2, s2w, gx * 32 - 16, gy * 64 - 32)
+    ra, rb = (l3.sweeps(x, None, PR) for x in (ra, rb))
+
     start2 = [prolong(r[40:72], t2s, p32) for r in (ra, rb, f2)]
-    after2 = start2
-    for _ in range(4):
-        after2 = [l2.sweep0(x) for x in after2]
+    after2 = [l2.sweeps(x, None, P2 * 2) for x in start2]
     h_of = [restrict(-l2.apply(x), t2s, r23) for x in after2]
     for n, h in enumerate(h_of):
         send3(h, 3 + n)
-    y2 = l2.sweep0(l2.sweep0(prolong(y3[40:72], t2s, p32)))
-    f5 = l1.sweep0(l1.sweep0(prolong(y2[8:56], t1s, p21)))
-    f5 = l1.sweep0(l1.sweep0(f5)) * (1.0 / 64)
-    ga, va, ta, ha = down2(4.0 * restrict(l1.apply(f5), t1s, rm))
-    ha = 4.0 * ha
-    send3(ha, 6)
-    f4 = l2.sweep0(l2.sweep0(y2)) * (1.0 / 16)
+    f4 = l2.sweeps(y2, None, P2) * (1.0 / 16)
     p4_of = [-dot2(f4, l2.apply(x)) for x in start2]
     p54 = -dot3(ha[8:24], f2[48:64])
+    z2 = l2.sweeps(start2[2], None, P2)
+    w1 = l1.sweeps(prolong(z2[8:56], t1s, p21), None, P1)
+    d1 = l1.sweeps(w1, None, P1)
+    h2, _, _, h3 = down2(restrict(-l1.apply(d1), t1s, rm))
+    send3(h3, 2)
+    send2(h2[16:48], 3)
 
     sum_next(0)
 
     g2w = join2(1)
-    kg2 = l2.k * g2w
-    v2 = l2.sweep(kg2, kg2)
+    kg2, v2, _ = l2.down(g2w)
     pv = dot1(f5, l1.residual(v1, g1)) - dot2(va, g2w)
     got(got_g.at[1], 96)
     G3 = g_line[...]
-    kg3 = l3.k * G3
-    v3 = l3.sweep(kg3, kg3)
-    kg4 = l4.k * restrict(l3.residual(v3, G3), t3s, r34)
-    e4 = kg4
-    for _ in range(11):
-        e4 = l4.sweep(e4, kg4)
-    x3 = v3 + prolong(e4, t3s, p43)
-    for _ in range(4):
-        x3 = l3.sweep(x3, kg3)
-    kg4 = l4.k * restrict(l3.residual(x3, G3), t3s, r34)
-    e4 = kg4
-    for _ in range(5):
-        e4 = l4.sweep(e4, kg4)
-    x3 = x3 + prolong(e4, t3s, p43)
-    for _ in range(2):
-        x3 = l3.sweep(x3, kg3)
+    kg3, v3, r3 = l3.down(G3)
+    kg4 = Moved(l4.k * restrict(r3, t3s, r34))
+    e4 = l4.sweeps(kg4, kg4, P4 * 5 + (1,))
+    x3 = l3.sweeps(v3 + prolong(e4, t3s, p43), kg3, P3 * 2)
+    kg4 = Moved(l4.k * restrict(l3.residual(x3, G3), t3s, r34))
+    e4 = l4.sweeps(kg4, kg4, P4 * 2 + (1,))
+    x3 = l3.sweeps(x3 + prolong(e4, t3s, p43), kg3, P3)
 
     x2 = v2 + prolong(x3[40:72], t2s, p32)
     p4 = dot2(f4, l2.residual(x2, g2w))
-    for _ in range(4):
-        x2 = l2.sweep(x2, kg2)
+    x2 = l2.sweeps(x2, kg2, P2 * 2)
     g3 = restrict(l2.residual(x2, g2w), t2s, r23)
     send3(g3, 0)
     ma = coarse(join3(*take3(6)))[8:24]
@@ -555,14 +644,6 @@
     sum_start(row, 1)
     tot = sum_end(0)
 
-    z2 = l2.sweep0(l2.sweep0(prolong(f2[40:72], t2s, p32)))
-    z1 = prolong(z2[8:56], t1s, p21)
-    w1 = l1.sweep0(l1.sweep0(z1))
-    d1 = l1.sweep0(l1.sweep0(w1))
-    h2, _, _, h3 = down2(restrict(-l1.apply(d1), t1s, rm))
-    send3(h3, 2)
-    send2(h2[16:48], 3)
-
     a1, a2, a3, ones_total, w6_total, qw12, qw6 = (pick(tot, n) for n in range(7))
     inv = 1.0 / ones_total
     c1 = a1 * inv
@@ -576,25 +657,22 @@
     parts = [take3(3 + n) for n in range(3)]
     G = [with_constants(b, p) for b, p in zip(take3(0), zip(*parts))]
     x2 = x2 + prolong(coarse(join3(*G)), t2s, p32)
-    for _ in range(2):
-        x2 = l2.sweep(x2, kg2)
+    x2 = l2.sweeps(x2, kg2, P2)
 
     x1 = v1 + prolong(x2[8:56], t1s, p21)
-    for _ in range(4):
-        x1 = l1.sweep(x1, kg1)
+    x1 = l1.sweeps(x1, kg1, P1 * 2)
     g2, _, _, g3 = down2(restrict(l1.residual(x1, g1), t1s, rm))
     send3(g3, 1)
     send2(g2[16:48], 2)
     sum_next(1)
     e3 = coarse(join3(*take3(2)))
     x2r = up2(e3, join2(3))
-    x1r = l1.sweep0(l1.sweep0(d1 + prolong(x2r[8:56], t1s, p21)))
+    x1r = l1.sweeps(d1 + prolong(x2r[8:56], t1s, p21), None, P1)
 
     e3 = coarse(join3(*take3(1)))
     x2 = up2(e3, join2(2))
     x1 = x1 + prolong(x2[8:56], t1s, p21)
-    for _ in range(2):
-        x1 = l1.sweep(x1, kg1)
+    x1 = l1.sweeps(x1, kg1, P1)
     tot = sum_end(1)
     b4, b41, b42, b43, b5, b51, b52, b53, b54 = (pick(tot, n) for n in range(9))
     c4 = with_constants(b4, (b41, b42, b43)) * inv
@@ -652,6 +730,8 @@
         + [v((4, 8, 32, 128), F32), v((4, 32, 128), F32)]
         + [v((7, 8, 8, 128), F32), v((7, 32, 128), F32), v((7, 2, 8, 128), F32)]
         + [v((2, 2, 1, 128), F32), v((2, 15, 1, 128), F32), v((2, 15, 1, 128), F32)]
+        + [v((2, 2, 32, 128), F32)] * 2
+        + [v((2, 4, 8, 128), F32)] * 2
         + [v((4096, 128), F32)]
         + [dma((1,)), dma((2,)), dma((2,)), dma((2,)), dma((4,)), dma((7,)), dma((2, 2)), dma((2,))]
     )

time: 46.9 us -> 44.3 us (0.945)
  Pallas kernels: 43 us -> 40.4 us
    pallas_call x1, Pallas kernels: 43 us -> 40.4 us  [body(): pl.pallas_call(kernel, out_shape=(shape, shape), in_specs=[pl.BlockSpec(m...]
where the time goes in v5:
time: 44.3 us; the launch traced here: 44.2 us
  Pallas kernels  40.4 us (91%)
  local copies, waits for them, and re-layouts  3.11 us (7%)
  between operations  0.65 us (1%)
    pallas_call x1, Pallas kernels, body(): pl.pallas_call(kernel, out_shape=(shape, shape), in_specs=[pl.BlockSpec(m...  40.4 us
    unnamed x6, local copies, waits for them, and re-layouts  3.11 us

profile of v5, /device:TPU:1, one launch (start us, length us, event | category | flops | bytes accessed | tf_op | source)
XLA Modules:
  0.0 44.2 jit_solution(11387605110420297029)
XLA Ops:
  0.6 0.0 copy-start
  0.6 0.9 %copy-done = f32[128,256]{1,0:T(8,128)S(1)} copy-done((f32[128,256]{1,0:T(8,128)S(1)}, f32[128,256]{1,0:T(8,128)}, u32[]{:S(2)}) %copy-start) | copy-done | bytes 131096
  1.5 0.0 copy-start.1
  1.5 0.9 %copy-done.1 = f32[128,256]{1,0:T(8,128)S(1)} copy-done((f32[128,256]{1,0:T(8,128)S(1)}, f32[128,256]{1,0:T(8,128)}, u32[]{:S(2)}) %copy-start.1) | copy-done | bytes 131096
  2.4 40.4 %fcycle.1 = (f32[128,256]{1,0:T(8,128)S(1)}, f32[128,256]{1,0:T(8,128)S(1)}) custom-call(f32[128,256]{1,0:T(8,128)S(1)} %copy-done, f32[128,256]{1,0:T(8,128)S(1)} %copy-done.1), custom_call_target="tpu_custom_call" | custom-call | tf_op jit(solution)/shard_map/fcycle/pallas_call | solution.py:740
  42.9 0.7 %copy.6 = f32[128,256]{1,0:T(8,128)} copy(f32[128,256]{1,0:T(8,128)S(1)} %get-tuple-element.4) | data formatting | bytes 262144
  43.5 0.7 %copy.7 = f32[128,256]{1,0:T(8,128)} copy(f32[128,256]{1,0:T(8,128)S(1)} %get-tuple-element.5) | data formatting | bytes 262144
Async XLA Ops:
  0.6 0.9 %copy-start = (f32[128,256]{1,0:T(8,128)S(1)}, f32[128,256]{1,0:T(8,128)}, u32[]{:S(2)}) copy-start(f32[128,256]{1,0:T(8,128)} %rhs_in.1) | copy-start | bytes 393220
  1.5 0.9 %copy-start.1 = (f32[128,256]{1,0:T(8,128)S(1)}, f32[128,256]{1,0:T(8,128)}, u32[]{:S(2)}) copy-start(f32[128,256]{1,0:T(8,128)} %shf_in.1) | copy-start | bytes 393220

commit v6 on v5

--- a/solution.py
+++ b/solution.py
@@ -578,6 +578,11 @@
     def dot3(a, b):
         return total(jnp.where(lane3, a * b, 0.0))
 
+    g_row = side_join(g3own, g_side, got_g)
+    ownb[1] = g_row
+    line_send(ownb.at[1], g_line, got_g)
+    g_line[48:64] = g_row
+
     s2w = join2(0)
     l2 = Level(2, s2w, gx * 32 - 16, gy * 64 - 32)
     y2 = l2.sweeps(prolong(y3[40:72], t2s, p32), None, P2)
@@ -585,11 +590,6 @@
     ga, va, ta, ha = down2(4.0 * restrict(l1.apply(f5), t1s, rm))
     ha = 4.0 * ha
     send3(ha, 6)
-
-    g_row = side_join(g3own, g_side, got_g)
-    ownb[1] = g_row
-    line_send(ownb.at[1], g_line, got_g)
-    g_line[48:64] = g_row
 
     ra, rb = prolong(w12, t3s, p43), prolong(w6, t3s, p43)
     ra, rb = (l3.sweeps(x, None, PR * 2) for x in (ra, rb))
@@ -606,13 +606,6 @@
     f4 = l2.sweeps(y2, None, P2) * (1.0 / 16)
     p4_of = [-dot2(f4, l2.apply(x)) for x in start2]
     p54 = -dot3(ha[8:24], f2[48:64])
-    z2 = l2.sweeps(start2[2], None, P2)
-    w1 = l1.sweeps(prolong(z2[8:56], t1s, p21), None, P1)
-    d1 = l1.sweeps(w1, None, P1)
-    h2, _, _, h3 = down2(restrict(-l1.apply(d1), t1s, rm))
-    send3(h3, 2)
-    send2(h2[16:48], 3)
-
     sum_next(0)
 
     g2w = join2(1)
@@ -643,6 +636,13 @@
         row = jnp.where(lane == n, p, row)
     sum_start(row, 1)
     tot = sum_end(0)
+
+    z2 = l2.sweeps(start2[2], None, P2)
+    w1 = l1.sweeps(prolong(z2[8:56], t1s, p21), None, P1)
+    d1 = l1.sweeps(w1, None, P1)
+    h2, _, _, h3 = down2(restrict(-l1.apply(d1), t1s, rm))
+    send3(h3, 2)
+    send2(h2[16:48], 3)
 
     a1, a2, a3, ones_total, w6_total, qw12, qw6 = (pick(tot, n) for n in range(7))
     inv = 1.0 / ones_total
@@ -711,6 +711,17 @@
         ],
         axis=1,
     )
+
+
+def store(a, b, out_a, out_b, sem):
+    copies = [
+        pltpu.make_async_copy(a, out_a, sem.at[0]),
+        pltpu.make_async_copy(b, out_b, sem.at[1]),
+    ]
+    for cp in copies:
+        cp.start()
+    for cp in copies:
+        cp.wait()
 
 
 def body(right_side, shift):
@@ -737,17 +748,27 @@
     )
     shape = jax.ShapeDtypeStruct((128, 256), F32)
     vm = pl.BlockSpec(memory_space=pltpu.VMEM)
-    return pl.pallas_call(
+    solved = pl.pallas_call(
         kernel,
-        out_shape=(shape, shape),
-        in_specs=[pl.BlockSpec(memory_space=pl.ANY)] * 2,
+        out_shape=(v((128, 256), F32),) * 2,
+        in_specs=[pl.BlockSpec(memory_space=pltpu.HBM)] * 2,
         out_specs=(vm, vm),
         scratch_shapes=scratch,
         compiler_params=pltpu.CompilerParams(
-            collective_id=0, has_side_effects=True, vmem_limit_bytes=40 * 1024 * 1024
+            collective_id=0, has_side_effects=True, vmem_limit_bytes=66428928
         ),
         name="fcycle",
     )(right_side, shift)
+    out = pl.BlockSpec(memory_space=pl.ANY)
+    return pl.pallas_call(
+        store,
+        out_shape=(shape, shape),
+        in_specs=[vm, vm],
+        out_specs=(out, out),
+        scratch_shapes=[dma((2,))],
+        compiler_params=pltpu.CompilerParams(vmem_limit_bytes=40 * 1024 * 1024),
+        name="store",
+    )(*solved)
 
 
 def solution(mesh):

time: 44.3 us -> 40.9 us (0.923)
  local copies, waits for them, and re-layouts: 3.11 us -> 0 us
    unnamed x6 -> x0, local copies, waits for them, and re-layouts: 3.11 us -> none
    pallas_call x1 -> x2, Pallas kernels: 40.4 us -> 40.2 us  [the longest x1 39.5 us: body(): pl.pallas_call(kernel, out_shape=(v((128, 256), F32),) * 2, in_specs=[pl....]
where the time goes in v6:
time: 40.9 us; the launch traced here: 40.8 us
  Pallas kernels  40.2 us (98%)
  between operations  0.64 us (2%)
    pallas_call x1, Pallas kernels, body(): pl.pallas_call(kernel, out_shape=(v((128, 256), F32),) * 2, in_specs=[pl....  39.5 us

profile of v6, /device:TPU:1, one launch (start us, length us, event | category | flops | bytes accessed | tf_op | source)
XLA Modules:
  0.0 40.8 jit_solution(10142471896279072333)
XLA Ops:
  0.6 39.5 %fcycle.1 = (f32[128,256]{1,0:T(8,128)S(1)}, f32[128,256]{1,0:T(8,128)S(1)}) custom-call(f32[128,256]{1,0:T(8,128)} %rhs_in.1, f32[128,256]{1,0:T(8,128)} %shf_in.1), custom_call_target="tpu_custom_call" | custom-call | tf_op jit(solution)/shard_map/fcycle/pallas_call | solution.py:751
  40.1 0.7 %store.1 = (f32[128,256]{1,0:T(8,128)}, f32[128,256]{1,0:T(8,128)}) custom-call(f32[128,256]{1,0:T(8,128)S(1)} %get-tuple-element.4.a, f32[128,256]{1,0:T(8,128)S(1)} %get-tuple-element.5.b), custom_call_target="tpu_custom_call" | custom-call | tf_op jit(solution)/shard_map/store/pallas_call | solution.py:763

commit v7 on v6

--- a/solution.py
+++ b/solution.py
@@ -15,8 +15,7 @@
 
 AROUND = [(-1, 0), (1, 0), (0, -1), (0, 1), (-1, -1), (-1, 1), (1, -1), (1, 1)]
 MIRROR = [1, 0, 3, 2, 7, 6, 5, 4]
-SIDE = [-1, 1, -2, 2]
-LINE = [-1, 1, -2, 2, -3, 3]
+WINDOW = [(dz, dy) for dz in range(-3, 4) for dy in range(-2, 3) if dz or dy]
 P1, P2, P3, P4 = (1, 1), (2,), (2,), (2,)
 PR, P3B, P4B = (1, 1), (2,), (3, 2)
 GROUP_A = [(dz, dc) for dz in range(8) for dc in range(2) if dz or dc]
@@ -140,10 +139,10 @@
     xg, xs, kk, kg0, v0, wa, wb, tmp0,
     t1s, t2s, t3s,
     rm, r23, r34, p43, p32, p21, r03,
-    s_side, s_line, g_side, g_line, own3, own3g, ownb,
+    win_in, win_out, window, own3,
     x2b, own2, x3b, own3n, own3p,
     ar_in, ar_a, ar_b,
-    edge_out, edge_in, corner_out, corner_in, rows_of, all_sent, got_border, got_s, got_g, got_2, got_3, got_sum, in_s,
+    edge_out, edge_in, corner_out, corner_in, rows_of, all_sent, got_border, got_window, got_2, got_3, got_sum, in_s,
 ):
     gx = lax.axis_index("gx")
     gy = lax.axis_index("gy")
@@ -167,11 +166,18 @@
             out = past(gy, dy, GY)
             return (gx + out * (other_row - gx), gy + (1 - out) * dy), out
         zo, yo = past(gx, dz, GX), past(gy, dy, GY)
-        high = lax.div(gx, 4)
-        if dz > 0:
-            ring = (1 - high) * other_row + high * (4 + lax.rem(gx, 3))
+        if dz % 2 == 0:
+            ring = other_row
+        elif dz > 0:
+            first = 5 - dz
+            high = lax.div(gx, first)
+            ring = (1 - lax.min(high, 1)) * other_row + lax.min(high, 1) * (
+                first + lax.rem(gx - first + 1 + 3 * 4, 3)
+            )
         else:
-            ring = high * other_row + (1 - high) * (1 + lax.rem(gx, 3))
+            first = -dz
+            high = lax.div(gx, first + 3)
+            ring = high * other_row + (1 - high) * (first + lax.rem(gx - first + 1 + 3 * 4, 3))
         to_z = zo * gx + (1 - zo) * (yo * ring + (1 - yo) * (gx + dz))
         to_y = zo * other_core + (1 - zo) * (yo * gy + (1 - yo) * (gy + dy))
         return (to_z, to_y), zo + (1 - zo) * yo
@@ -187,7 +193,7 @@
 
     barrier = pltpu.get_barrier_semaphore()
     partners = (
-        [beyond(*o)[0] for o in AROUND]
+        [beyond(*o)[0] for o in WINDOW]
         + [in_a(*o) for o in GROUP_A]
         + [in_b(*o) for o in GROUP_B]
     )
@@ -346,25 +352,35 @@
                         keep, shifted(p, at - 32 * n), 0.0
                     )
 
-    def side_send(src, buf, sem):
-        for n, d in enumerate(SIDE):
-            dev, out = beyond(0, d)
-            send(src, buf.at[slot(n, n ^ 1, out)], sem.at[0], dev)
-
-    def side_join(own, buf, sem):
-        got(sem.at[0], 64)
-        right1, left1, right2, left2 = (buf[n] for n in range(4))
-        lane = iota((16, 128), 1)
-        out = jnp.where(lane < 48, pltpu.roll(left1, 96, axis=1), own)
-        out = jnp.where(lane < 16, pltpu.roll(left2, 64, axis=1), out)
-        out = jnp.where(lane >= 80, pltpu.roll(right1, 32, axis=1), out)
-        return jnp.where(lane >= 112, pltpu.roll(right2, 64, axis=1), out)
-
-    def line_send(src, buf, sem):
-        for d in LINE:
-            dev, out = beyond(d, 0)
-            at = pl.ds(pl.multiple_of(16 * slot(3 - d, 3 + d, out), 8), 16)
-            send(src, buf.at[at], sem.at[1], dev)
+    def pack_window(x):
+        a, b = x[0:8], x[8:16]
+        lane = iota((8, 128), 1)
+        out = jnp.where(
+            lane < 96, shifted(b, 16), shifted(pltpu.roll(b, 4, axis=0), 48)
+        )
+        out = jnp.where(lane < 64, shifted(pltpu.roll(a, 4, axis=0), -16), out)
+        return jnp.where(lane < 32, shifted(a, -48), out)[0:4]
+
+    def spread(k, x):
+        p = pack_window(x)
+        win_out[k] = p
+        win_in[k, 3, 2] = p
+        for dz, dy in WINDOW:
+            dev, out = beyond(dz, dy)
+            at = win_in.at[k, 3 - dz + 2 * dz * out, 2 - dy + 2 * dy * out]
+            send(win_out.at[k], at, got_window.at[k], dev)
+
+    def collect(k):
+        got(got_window.at[k], 4 * len(WINDOW))
+        lane = iota((4, 128), 1)
+        for r in range(7):
+            for q in range(4):
+                out = shifted(win_in[k, r, 0], -16 - 32 * q)
+                for c in range(1, 5):
+                    at = 32 * c - 16
+                    out = jnp.where(lane < at, out, shifted(win_in[k, r, c], at - 32 * q))
+                window[k, 16 * r + 4 * q : 16 * r + 4 * q + 4, :] = out
+        return window[k]
 
     SRC2 = {-1: (0, 16), 1: (16, 32), 0: (0, 32)}
 
@@ -443,14 +459,10 @@
         got(got_sum.at[k, 1], 15)
         return ar_in[k, 1] + jnp.sum(ar_b[k], axis=0)
 
-    side_send(own3, s_side, got_s)
     border_rows = border(1)
     border(0)
+    spread(0, own3[...])
     send2(own2[0], 0)
-    s_row = side_join(own3[...], s_side, got_s)
-    ownb[0] = s_row
-    line_send(ownb.at[0], s_line, got_s)
-    s_line[48:64] = s_row
 
     row0 = gx * 128 - 32
     col0 = gy * 256 - 128
@@ -506,13 +518,12 @@
     _, _, r2 = l2a.down(g2)
     g3 = restrict(r2, t2s, r23)
     g3own = g3[4:20]
-    own3g[...] = g3own
-    side_send(own3g, g_side, got_g)
+    spread(1, g3own)
     send2(g2[8:40], 1)
 
-    got(got_s.at[1], 96)
-    l3 = Level(3, s_line[...], gx * 16 - 48, gy * 32 - 48)
-    s4 = restrict(s_line[...], t3s, r34)
+    s_window = collect(0)
+    l3 = Level(3, s_window, gx * 16 - 48, gy * 32 - 48)
+    s4 = restrict(s_window, t3s, r34)
     l4 = Level(4, s4, gx * 8 - 24, gy * 16 - 24, iota((56, 128), 1) < 64)
 
     one4 = jnp.where(l4.ok, 1.0, 0.0)
@@ -578,11 +589,6 @@
     def dot3(a, b):
         return total(jnp.where(lane3, a * b, 0.0))
 
-    g_row = side_join(g3own, g_side, got_g)
-    ownb[1] = g_row
-    line_send(ownb.at[1], g_line, got_g)
-    g_line[48:64] = g_row
-
     s2w = join2(0)
     l2 = Level(2, s2w, gx * 32 - 16, gy * 64 - 32)
     y2 = l2.sweeps(prolong(y3[40:72], t2s, p32), None, P2)
@@ -606,16 +612,15 @@
     f4 = l2.sweeps(y2, None, P2) * (1.0 / 16)
     p4_of = [-dot2(f4, l2.apply(x)) for x in start2]
     p54 = -dot3(ha[8:24], f2[48:64])
-    sum_next(0)
 
     g2w = join2(1)
     kg2, v2, _ = l2.down(g2w)
     pv = dot1(f5, l1.residual(v1, g1)) - dot2(va, g2w)
-    got(got_g.at[1], 96)
-    G3 = g_line[...]
+    G3 = collect(1)
     kg3, v3, r3 = l3.down(G3)
     kg4 = Moved(l4.k * restrict(r3, t3s, r34))
     e4 = l4.sweeps(kg4, kg4, P4 * 5 + (1,))
+    sum_next(0)
     x3 = l3.sweeps(v3 + prolong(e4, t3s, p43), kg3, P3 * 2)
     kg4 = Moved(l4.k * restrict(l3.residual(x3, G3), t3s, r34))
     e4 = l4.sweeps(kg4, kg4, P4 * 2 + (1,))
@@ -635,7 +640,7 @@
     for n, p in enumerate([p4, *p4_of, p5, *p5_of, p54]):
         row = jnp.where(lane == n, p, row)
     sum_start(row, 1)
-    tot = sum_end(0)
+    parts = [take3(3 + n) for n in range(3)]
 
     z2 = l2.sweeps(start2[2], None, P2)
     w1 = l1.sweeps(prolong(z2[8:56], t1s, p21), None, P1)
@@ -644,6 +649,7 @@
     send3(h3, 2)
     send2(h2[16:48], 3)
 
+    tot = sum_end(0)
     a1, a2, a3, ones_total, w6_total, qw12, qw6 = (pick(tot, n) for n in range(7))
     inv = 1.0 / ones_total
     c1 = a1 * inv
@@ -654,7 +660,6 @@
         return ((x + c1 * parts[0]) + c2 * parts[1]) + c3 * parts[2]
 
     x2 = with_constants(x2, after2)
-    parts = [take3(3 + n) for n in range(3)]
     G = [with_constants(b, p) for b, p in zip(take3(0), zip(*parts))]
     x2 = x2 + prolong(coarse(join3(*G)), t2s, p32)
     x2 = l2.sweeps(x2, kg2, P2)
@@ -735,16 +740,15 @@
         + [v((256, 128), BF16)]
         + [v((128, 128), BF16)] * 4
         + [v((128, 256), BF16), v((256, 128), BF16)]
-        + [v((4, 16, 128), F32), v((112, 128), F32)] * 2
-        + [v((16, 128), F32)] * 2
-        + [v((2, 16, 128), F32)]
+        + [v((2, 7, 5, 4, 128), F32), v((2, 4, 128), F32), v((2, 112, 128), F32)]
+        + [v((16, 128), F32)]
         + [v((4, 8, 32, 128), F32), v((4, 32, 128), F32)]
         + [v((7, 8, 8, 128), F32), v((7, 32, 128), F32), v((7, 2, 8, 128), F32)]
         + [v((2, 2, 1, 128), F32), v((2, 15, 1, 128), F32), v((2, 15, 1, 128), F32)]
         + [v((2, 2, 32, 128), F32)] * 2
         + [v((2, 4, 8, 128), F32)] * 2
         + [v((4096, 128), F32)]
-        + [dma((1,)), dma((2,)), dma((2,)), dma((2,)), dma((4,)), dma((7,)), dma((2, 2)), dma((2,))]
+        + [dma((1,)), dma((2,)), dma((2,)), dma((4,)), dma((7,)), dma((2, 2)), dma((2,))]
     )
     shape = jax.ShapeDtypeStruct((128, 256), F32)
     vm = pl.BlockSpec(memory_space=pltpu.VMEM)

time: 40.9 us -> 39.9 us (0.976)
  Pallas kernels: 40.2 us -> 39.2 us
    pallas_call x1, Pallas kernels: 39.5 us -> 38.5 us  [body(): pl.pallas_call(kernel, out_shape=(v((128, 256), F32),) * 2, in_specs=[pl....]
where the time goes in v7:
time: 39.9 us; the launch traced here: 39.8 us
  Pallas kernels  39.2 us (98%)
  between operations  0.64 us (2%)
    pallas_call x1, Pallas kernels, body(): pl.pallas_call(kernel, out_shape=(v((128, 256), F32),) * 2, in_specs=[pl....  38.5 us

profile of v7, /device:TPU:1, one launch (start us, length us, event | category | flops | bytes accessed | tf_op | source)
XLA Modules:
  0.0 39.8 jit_solution(3854459106301953658)
XLA Ops:
  0.6 38.5 %fcycle.1 = (f32[128,256]{1,0:T(8,128)S(1)}, f32[128,256]{1,0:T(8,128)S(1)}) custom-call(f32[128,256]{1,0:T(8,128)} %rhs_in.1, f32[128,256]{1,0:T(8,128)} %shf_in.1), custom_call_target="tpu_custom_call" | custom-call | tf_op jit(solution)/shard_map/fcycle/pallas_call | solution.py:755
  39.1 0.7 %store.1 = (f32[128,256]{1,0:T(8,128)}, f32[128,256]{1,0:T(8,128)}) custom-call(f32[128,256]{1,0:T(8,128)S(1)} %get-tuple-element.4.a, f32[128,256]{1,0:T(8,128)S(1)} %get-tuple-element.5.b), custom_call_target="tpu_custom_call" | custom-call | tf_op jit(solution)/shard_map/store/pallas_call | solution.py:767
